TPU v7x, 32 devices: a whole 2x2x4 slice. The times are simulated.
32 devices in a mesh: shard: 4 (over y, x), ctx: 8 (over z, core).
Axes of the slice: x: 2, y: 2, z: 4, core: 2. Of those that a mesh axis runs over, the one named last changes fastest.
Arguments:
- layer_input: bfloat16 [4, 1024, 768], P('shard', 'ctx'), may hold values from -6 to 6
- positions: int32 [4, 1024], P('shard', 'ctx'), may hold values from 0 to 1023, as said below
- cotangent: bfloat16 [4, 1024, 768], P('shard', 'ctx'), may hold values from -6 to 6
- ln1_gain: float32 [768], replicated, may hold values from 0.5 to 1.5
- ln1_bias: float32 [768], replicated, may hold values from -3 to 3
- ln2_gain: float32 [768], replicated, may hold values from 0.5 to 1.5
- ln2_bias: float32 [768], replicated, may hold values from -3 to 3
- w_qkv: bfloat16 [768, 2304], P('shard')
- qkv_bias: float32 [2304], replicated, may hold values from -3 to 3
- w_out: bfloat16 [768, 768], P('shard'), may hold values from -1.25 to 1.25
- w_up: bfloat16 [768, 3072], P('shard'), may hold values from -0.21875 to 0.21875
- up_bias: float32 [3072], replicated, may hold values from -3 to 3
- w_down: bfloat16 [3072, 768], P('shard'), may hold values from -0.109375 to 0.109375
Outputs:
- layer_output: bfloat16 [4, 1024, 768], P('shard', 'ctx')
- grad_input: bfloat16 [4, 1024, 768], P('shard', 'ctx')
- grad_ln1_gain: float32 [768], replicated
- grad_ln1_bias: float32 [768], replicated
- grad_ln2_gain: float32 [768], replicated
- grad_ln2_bias: float32 [768], replicated
- grad_w_qkv: float32 [768, 2304], P('shard')
- grad_qkv_bias: float32 [2304], replicated
- grad_w_out: float32 [768, 768], P('shard')
- grad_w_up: float32 [768, 3072], P('shard')
- grad_up_bias: float32 [3072], replicated
- grad_w_down: float32 [3072, 768], P('shard')
Inputs may be any that keep to these rules, and one draw needn't show every extreme that they name: In each sequence, the 128 tokens that one device holds along ctx carry consecutive positions starting at a multiple of 128; every position of the sequence occurs once.
All inputs are finite; a program needn't handle non-finite values.
Results may differ from a plain program's by a relative error of at most 0.018.
Values may be sent and summed in bfloat16 or wider, within the bound.
A program may use at most 128 MiB of HBM per device.

v0:
```python
import jax
import jax.numpy as jnp
from jax import lax
from jax.sharding import PartitionSpec as P

HEADS = 12
HEAD_DIM = 64
ROTARY = 16


EPSILON = 1e-05
NEGATIVE = -1e30


def shifted(shard, axis, by):
    count = lax.axis_size(axis)
    return lax.ppermute(shard, axis, [(i, (i + by) % count) for i in range(count)])


def layer_norm(values_in, gain_vec, bias_vec):
    centered = values_in - jnp.mean(values_in, axis=-1, keepdims=True)
    variance = jnp.mean(centered * centered, axis=-1, keepdims=True)
    return centered * lax.rsqrt(variance + EPSILON) * gain_vec + bias_vec


def rotary_tables(position_ids):
    half_dim = ROTARY // 2
    inverse_freq = 1.0 / 10000.0 ** (jnp.arange(half_dim, dtype=jnp.float32) * (2.0 / ROTARY))
    angles = position_ids.astype(jnp.float32)[..., None] * inverse_freq
    return (jnp.cos(angles), jnp.sin(angles))


def rotate(field_in, cosine, sine_table):
    half_dim = cosine.shape[-1]
    lead_part = field_in[..., :half_dim]
    second = field_in[..., half_dim : 2 * half_dim]
    remain = field_in[..., 2 * half_dim :]
    cos_wide = cosine[..., None, :]
    sin_wide = sine_table[..., None, :]
    return jnp.concatenate(
        [
            lead_part * cos_wide - second * sin_wide,
            second * cos_wide + lead_part * sin_wide,
            remain,
        ],
        axis=-1,
    )


def gelu_exact(field_in):
    return jax.nn.gelu(field_in, approximate=False)


def on_device(
    layer_input,
    positions,
    cotangent,
    ln1_gain,
    ln1_bias,
    ln2_gain,
    ln2_bias,
    w_qkv,
    qkv_bias,
    w_out,
    w_up,
    up_bias,
    w_down,
):
    seqs_here, block_len, feature_count = layer_input.shape
    row_count = seqs_here * block_len
    head_count = HEADS
    head_size = HEAD_DIM
    score_scale = head_size ** (-0.5)
    whole_qkv, whole_out, whole_up, whole_down = (
        lax.all_gather(w_qkv, "shard", axis=0, tiled=True),
        lax.all_gather(w_out, "shard", axis=0, tiled=True),
        lax.all_gather(w_up, "shard", axis=0, tiled=True),
        lax.all_gather(w_down, "shard", axis=0, tiled=True),
    )
    all_positions = lax.all_gather(positions, "ctx", axis=1, tiled=True)
    cycle_size = lax.axis_size("ctx")
    my_index = lax.axis_index("ctx")
    inputs = layer_input.astype(jnp.float32).reshape(row_count, feature_count)
    normed_one = layer_norm(inputs, ln1_gain, ln1_bias).astype(jnp.bfloat16)
    normed_two = layer_norm(inputs, ln2_gain, ln2_bias).astype(jnp.bfloat16)
    projected = jnp.dot(normed_one, whole_qkv, preferred_element_type=jnp.float32) + qkv_bias
    split_heads = projected.reshape(seqs_here, block_len, 3, head_count, head_size)
    cosine, sine_table = rotary_tables(positions)
    queries = rotate(split_heads[:, :, 0], cosine, sine_table).astype(jnp.bfloat16)
    key_rows = rotate(split_heads[:, :, 1], cosine, sine_table).astype(jnp.bfloat16)
    value_rows = split_heads[:, :, 2].astype(jnp.bfloat16)
    top_query = jnp.max(positions)

    def attend_block(running, key_blk, value_blk, key_pos):

        def attend_update(current):
            run_max, run_sum, run_acc = current
            scores = (
                jnp.einsum("sqhd,skhd->shqk", queries, key_blk, preferred_element_type=jnp.float32)
                * score_scale
            )
            allowed = key_pos[:, None, None, :] <= positions[:, None, :, None]
            masked = jnp.where(allowed, scores, NEGATIVE)
            new_max = jnp.maximum(run_max, jnp.max(masked, axis=-1))
            shrink = jnp.exp(run_max - new_max)
            weights_now = jnp.where(allowed, jnp.exp(masked - new_max[..., None]), 0.0)
            run_sum = run_sum * shrink + jnp.sum(weights_now, axis=-1)
            added_term = jnp.einsum(
                "shqk,skhd->sqhd",
                weights_now.astype(jnp.bfloat16),
                value_blk,
                preferred_element_type=jnp.float32,
            )
            run_acc = run_acc * jnp.transpose(shrink, (0, 2, 1))[..., None] + added_term
            return (new_max, run_sum, run_acc)

        return lax.cond(
            jnp.min(key_pos) <= top_query, attend_update, lambda unchanged: unchanged, running
        )

    initial = (
        jnp.full((seqs_here, head_count, block_len), NEGATIVE, jnp.float32),
        jnp.zeros((seqs_here, head_count, block_len), jnp.float32),
        jnp.zeros((seqs_here, block_len, head_count, head_size), jnp.float32),
    )
    own_block = attend_block(initial, key_rows, value_rows, positions)

    def cycle_forward(turn_index, carried):
        current, key_cur, value_cur = carried
        key_cur, value_cur = shifted((key_cur, value_cur), "ctx", 1)
        source = (my_index - turn_index) % cycle_size
        key_pos = lax.dynamic_slice_in_dim(all_positions, source * block_len, block_len, 1)
        return (attend_block(current, key_cur, value_cur, key_pos), key_cur, value_cur)

    (run_max, run_sum, run_acc), unused_key, unused_value = lax.fori_loop(
        1, cycle_size, cycle_forward, (own_block, key_rows, value_rows)
    )
    attn_vals = run_acc / jnp.transpose(run_sum, (0, 2, 1))[..., None]
    log_total = run_max + jnp.log(run_sum)
    attn_low = attn_vals.astype(jnp.bfloat16).reshape(row_count, feature_count)
    attn_branch = jnp.dot(attn_low, whole_out, preferred_element_type=jnp.float32)
    hidden_pre = jnp.dot(normed_two, whole_up, preferred_element_type=jnp.float32) + up_bias
    hidden_low = gelu_exact(hidden_pre).astype(jnp.bfloat16)
    mlp_branch = jnp.dot(hidden_low, whole_down, preferred_element_type=jnp.float32)
    layer_output = (
        (inputs + attn_branch + mlp_branch)
        .astype(jnp.bfloat16)
        .reshape(seqs_here, block_len, feature_count)
    )
    cot_low = cotangent.reshape(row_count, feature_count)
    cot_full = cot_low.astype(jnp.float32)
    grad_down = jnp.einsum("rf,rd->fd", hidden_low, cot_low, preferred_element_type=jnp.float32)
    grad_hidden = jnp.einsum("rd,fd->rf", cot_low, whole_down, preferred_element_type=jnp.float32)
    unused_gelu, gelu_back = jax.vjp(gelu_exact, hidden_pre)
    grad_pre = gelu_back(grad_hidden)[0].astype(jnp.bfloat16)
    grad_up_bias = jnp.sum(grad_pre.astype(jnp.float32), axis=0)
    grad_up = jnp.einsum("rd,rf->df", normed_two, grad_pre, preferred_element_type=jnp.float32)
    grad_two = jnp.einsum("rf,df->rd", grad_pre, whole_up, preferred_element_type=jnp.float32)
    grad_out = jnp.einsum("rd,re->de", attn_low, cot_low, preferred_element_type=jnp.float32)
    grad_attn = (
        jnp.einsum("re,de->rd", cot_low, whole_out, preferred_element_type=jnp.float32)
        .astype(jnp.bfloat16)
        .reshape(seqs_here, block_len, head_count, head_size)
    )
    row_delta = jnp.transpose(
        jnp.sum(grad_attn.astype(jnp.float32) * attn_vals, axis=-1), (0, 2, 1)
    )

    def back_block(grads_in, key_blk, value_blk, key_pos):

        def back_update(current):
            grad_query, grad_key, grad_value = current
            scores = (
                jnp.einsum("sqhd,skhd->shqk", queries, key_blk, preferred_element_type=jnp.float32)
                * score_scale
            )
            allowed = key_pos[:, None, None, :] <= positions[:, None, :, None]
            masked = jnp.where(allowed, scores, NEGATIVE)
            probability = jnp.exp(masked - log_total[..., None])
            prob_low = probability.astype(jnp.bfloat16)
            grad_value = grad_value + jnp.einsum(
                "shqk,sqhd->skhd", prob_low, grad_attn, preferred_element_type=jnp.float32
            )
            grad_prob = jnp.einsum(
                "sqhd,skhd->shqk", grad_attn, value_blk, preferred_element_type=jnp.float32
            )
            grad_score = (probability * (grad_prob - row_delta[..., None])).astype(jnp.bfloat16)
            grad_query = (
                grad_query
                + jnp.einsum(
                    "shqk,skhd->sqhd", grad_score, key_blk, preferred_element_type=jnp.float32
                )
                * score_scale
            )
            grad_key = (
                grad_key
                + jnp.einsum(
                    "shqk,sqhd->skhd", grad_score, queries, preferred_element_type=jnp.float32
                )
                * score_scale
            )
            return (grad_query, grad_key, grad_value)

        return lax.cond(
            jnp.min(key_pos) <= top_query, back_update, lambda unchanged: unchanged, grads_in
        )

    zero_rows = jnp.zeros((seqs_here, block_len, head_count, head_size), jnp.float32)

    def pass_back(grad_key, grad_value):
        return (
            shifted(grad_key.astype(jnp.bfloat16), "ctx", 1).astype(grad_key.dtype),
            shifted(grad_value.astype(jnp.bfloat16), "ctx", 1).astype(grad_value.dtype),
        )

    grad_query, grad_key, grad_value = back_block(
        (zero_rows, zero_rows, zero_rows), key_rows, value_rows, positions
    )
    grad_key, grad_value = pass_back(grad_key, grad_value)

    def cycle_backward(turn_index, carried):
        grad_query, key_cur, value_cur, grad_key, grad_value = carried
        key_cur, value_cur = shifted((key_cur, value_cur), "ctx", 1)
        source = (my_index - turn_index) % cycle_size
        key_pos = lax.dynamic_slice_in_dim(all_positions, source * block_len, block_len, 1)
        grad_query, grad_key, grad_value = back_block(
            (grad_query, grad_key, grad_value), key_cur, value_cur, key_pos
        )
        grad_key, grad_value = pass_back(grad_key, grad_value)
        return (grad_query, key_cur, value_cur, grad_key, grad_value)

    grad_query, unused_key, unused_value, grad_key, grad_value = lax.fori_loop(
        1, cycle_size, cycle_backward, (grad_query, key_rows, value_rows, grad_key, grad_value)
    )
    unused_rot, rotate_back = jax.vjp(
        lambda field_in: rotate(field_in, cosine, sine_table), zero_rows
    )
    query_pre = rotate_back(grad_query)[0]
    key_pre = rotate_back(grad_key)[0]
    grad_proj = (
        jnp.stack([query_pre, key_pre, grad_value], axis=2)
        .reshape(row_count, 3 * feature_count)
        .astype(jnp.bfloat16)
    )
    grad_qkv_bias = jnp.sum(grad_proj.astype(jnp.float32), axis=0)
    grad_qkv = jnp.einsum("rd,re->de", normed_one, grad_proj, preferred_element_type=jnp.float32)
    grad_one = jnp.einsum("re,de->rd", grad_proj, whole_qkv, preferred_element_type=jnp.float32)
    unused_one, norm_back_one = jax.vjp(layer_norm, inputs, ln1_gain, ln1_bias)
    input_one, grad_gain_one, grad_bias_one = norm_back_one(grad_one)
    unused_two, norm_back_two = jax.vjp(layer_norm, inputs, ln2_gain, ln2_bias)
    input_two, grad_gain_two, grad_bias_two = norm_back_two(grad_two)
    grad_input = (
        (cot_full + input_one + input_two)
        .astype(jnp.bfloat16)
        .reshape(seqs_here, block_len, feature_count)
    )
    summed = (
        lax.psum(grad_qkv.astype(jnp.bfloat16), "ctx").astype(jnp.float32),
        lax.psum(grad_out.astype(jnp.bfloat16), "ctx").astype(jnp.float32),
        lax.psum(grad_up.astype(jnp.bfloat16), "ctx").astype(jnp.float32),
        lax.psum(grad_down.astype(jnp.bfloat16), "ctx").astype(jnp.float32),
        lax.psum(grad_gain_one.astype(jnp.bfloat16), "ctx").astype(jnp.float32),
        lax.psum(grad_bias_one.astype(jnp.bfloat16), "ctx").astype(jnp.float32),
        lax.psum(grad_gain_two.astype(jnp.bfloat16), "ctx").astype(jnp.float32),
        lax.psum(grad_bias_two.astype(jnp.bfloat16), "ctx").astype(jnp.float32),
        lax.psum(grad_qkv_bias.astype(jnp.bfloat16), "ctx").astype(jnp.float32),
        lax.psum(grad_up_bias.astype(jnp.bfloat16), "ctx").astype(jnp.float32),
    )
    sum_qkv, sum_out, sum_up, sum_down = (
        lax.psum_scatter(
            summed[0].astype(jnp.bfloat16), "shard", scatter_dimension=0, tiled=True
        ).astype(jnp.float32),
        lax.psum_scatter(
            summed[1].astype(jnp.bfloat16), "shard", scatter_dimension=0, tiled=True
        ).astype(jnp.float32),
        lax.psum_scatter(
            summed[2].astype(jnp.bfloat16), "shard", scatter_dimension=0, tiled=True
        ).astype(jnp.float32),
        lax.psum_scatter(
            summed[3].astype(jnp.bfloat16), "shard", scatter_dimension=0, tiled=True
        ).astype(jnp.float32),
    )
    sum_small = (
        lax.psum(summed[4].astype(jnp.bfloat16), "shard").astype(jnp.float32),
        lax.psum(summed[5].astype(jnp.bfloat16), "shard").astype(jnp.float32),
        lax.psum(summed[6].astype(jnp.bfloat16), "shard").astype(jnp.float32),
        lax.psum(summed[7].astype(jnp.bfloat16), "shard").astype(jnp.float32),
        lax.psum(summed[8].astype(jnp.bfloat16), "shard").astype(jnp.float32),
        lax.psum(summed[9].astype(jnp.bfloat16), "shard").astype(jnp.float32),
    )
    return (
        layer_output,
        grad_input,
        sum_small[0],
        sum_small[1],
        sum_small[2],
        sum_small[3],
        sum_qkv,
        sum_small[4],
        sum_out,
        sum_up,
        sum_small[5],
        sum_down,
    )


def solution(mesh):
    placed = (
        P("shard", "ctx", None),
        P("shard", "ctx"),
        P("shard", "ctx", None),
        P(),
        P(),
        P(),
        P(),
        P("shard", None),
        P(),
        P("shard", None),
        P("shard", None),
        P(),
        P("shard", None),
    )
    return jax.shard_map(
        on_device,
        mesh=mesh,
        in_specs=placed,
        out_specs=(
            P("shard", "ctx", None),
            P("shard", "ctx", None),
            P(),
            P(),
            P(),
            P(),
            P("shard", None),
            P(),
            P("shard", None),
            P("shard", None),
            P(),
            P("shard", None),
        ),
        check_vma=False,
    )
```

profile of v0, /device:TPU:0, one launch (start us, length us, event | category | flops | bytes accessed | tf_op | source)
XLA Modules:
  0.0 602.1 jit_solution(3301122409901663954)
XLA Ops:
  12.0 14.1 %all_gather.16 = s32[1,1024]{1,0:T(1,128)} all-gather(s32[1,128]{1,0:T(1,128)S(1)} %copy-done.10), channel_id=1, replica_groups=mesh['shard'=4,'ctx'=8] {'ctx'}, dimensions={1}, use_global_device_ids=true | all-gather | bytes 4608 | tf_op jit(solution)/shard_map/all_gather | solution.py:80
  27.0 13.2 %all-gather.7.cloned.1.call-done = bf16[768,768]{1,0:T(8,128)(2,1)} async-done(((bf16[192,768]{1,0:T(8,128)(2,1)}), bf16[768,768]{1,0:T(8,128)(2,1)}) %all-gather.7.cloned.1.call-update) | async-done | bytes 1179664 | tf_op jit(solution)/shard_map/all_gather | solution.py:76
  42.1 47.0 %all-gather.5.cloned.1.call-done = bf16[768,2304]{1,0:T(8,128)(2,1)} async-done(((bf16[192,2304]{1,0:T(8,128)(2,1)}), bf16[768,2304]{1,0:T(8,128)(2,1)}) %all-gather.5.cloned.1.call-update) | async-done | bytes 3538960 | tf_op jit(solution)/shard_map/all_gather | solution.py:75
  94.8 72.4 %while.46 = (s32[]{:T(128)}, f32[1,12,128]{2,1,0:T(8,128)}, f32[1,12,128]{2,1,0:T(8,128)S(1)}, f32[1,128,12,64]{1,3,2,0:T(8,128)S(1)}, bf16[1,128,12,64]{1,3,2,0...) while((s32[]{:T(128)}, f32[1,12,128]{2,1,0:T(8,128)}, ...), condition=%wide.region_14.15_spmd, body=%wide.region_8.14_spmd.sunk | while | flops 52318864 | bytes 6261282 | solution.py:135
  130.6 4.2 collective-permute-done.1
  171.6 6.8 %collective-permute-done.7 = bf16[1,128,12,64]{1,3,2,0:T(8,128)(2,1)S(1)} collective-permute-done((bf16[1,128,12,64]{1,3,2,0:T(8,128)(2,1)S(1)}, bf16[1,128,12,64]{1,3,2,0:T(8,128)(2,1)S(1)}, u32[]{:S(2)}, u32[]{:S(2)}) %collective-permute-start.7) | collective-permute-done | bytes 196640 | tf_op jit(solution)/shard_map/ppermute | solution.py:17
  180.5 132.8 %while.47 = (s32[]{:T(128)}, f32[1,128,12,64]{1,3,2,0:T(8,128)S(1)}, bf16[1,128,12,64]{1,3,2,0:T(8,128)(2,1)S(1)}, bf16[1,128,12,64]{1,3,2,0:T(8,128)(2,1)S(1)},...) while((s32[]{:T(128)}, ...), condition=%wide.region_22.23_spmd, body=%wide.region_18.0_spmd.sunk | while | flops 128106640 | bytes 13613730 | solution.py:232
  183.2 4.3 collective-permute-done.3
  191.7 6.7 %collective-permute-done.5 = bf16[1,128,12,64]{1,3,2,0:T(8,128)(2,1)S(1)} collective-permute-done((bf16[1,128,12,64]{1,3,2,0:T(8,128)(2,1)S(1)}, bf16[1,128,12,64]{1,3,2,0:T(8,128)(2,1)S(1)}, u32[]{:S(2)}, u32[]{:S(2)}) %collective-permute-start.5) | collective-permute-done | bytes 196640 | tf_op jit(solution)/shard_map/while/body/eval_jaxpr/ppermute | solution.py:17
  211.7 6.7 %collective-permute-done.5 = bf16[1,128,12,64]{1,3,2,0:T(8,128)(2,1)S(1)} collective-permute-done((bf16[1,128,12,64]{1,3,2,0:T(8,128)(2,1)S(1)}, bf16[1,128,12,64]{1,3,2,0:T(8,128)(2,1)S(1)}, u32[]{:S(2)}, u32[]{:S(2)}) %collective-permute-start.5) | collective-permute-done | bytes 196640 | tf_op jit(solution)/shard_map/while/body/eval_jaxpr/ppermute | solution.py:17
  229.9 6.7 %collective-permute-done.5 = bf16[1,128,12,64]{1,3,2,0:T(8,128)(2,1)S(1)} collective-permute-done((bf16[1,128,12,64]{1,3,2,0:T(8,128)(2,1)S(1)}, bf16[1,128,12,64]{1,3,2,0:T(8,128)(2,1)S(1)}, u32[]{:S(2)}, u32[]{:S(2)}) %collective-permute-start.5) | collective-permute-done | bytes 196640 | tf_op jit(solution)/shard_map/while/body/eval_jaxpr/ppermute | solution.py:17
  248.1 6.7 %collective-permute-done.5 = bf16[1,128,12,64]{1,3,2,0:T(8,128)(2,1)S(1)} collective-permute-done((bf16[1,128,12,64]{1,3,2,0:T(8,128)(2,1)S(1)}, bf16[1,128,12,64]{1,3,2,0:T(8,128)(2,1)S(1)}, u32[]{:S(2)}, u32[]{:S(2)}) %collective-permute-start.5) | collective-permute-done | bytes 196640 | tf_op jit(solution)/shard_map/while/body/eval_jaxpr/ppermute | solution.py:17
  266.3 6.7 %collective-permute-done.5 = bf16[1,128,12,64]{1,3,2,0:T(8,128)(2,1)S(1)} collective-permute-done((bf16[1,128,12,64]{1,3,2,0:T(8,128)(2,1)S(1)}, bf16[1,128,12,64]{1,3,2,0:T(8,128)(2,1)S(1)}, u32[]{:S(2)}, u32[]{:S(2)}) %collective-permute-start.5) | collective-permute-done | bytes 196640 | tf_op jit(solution)/shard_map/while/body/eval_jaxpr/ppermute | solution.py:17
  286.3 6.7 %collective-permute-done.5 = bf16[1,128,12,64]{1,3,2,0:T(8,128)(2,1)S(1)} collective-permute-done((bf16[1,128,12,64]{1,3,2,0:T(8,128)(2,1)S(1)}, bf16[1,128,12,64]{1,3,2,0:T(8,128)(2,1)S(1)}, u32[]{:S(2)}, u32[]{:S(2)}) %collective-permute-start.5) | collective-permute-done | bytes 196640 | tf_op jit(solution)/shard_map/while/body/eval_jaxpr/ppermute | solution.py:17
  304.5 6.7 %collective-permute-done.5 = bf16[1,128,12,64]{1,3,2,0:T(8,128)(2,1)S(1)} collective-permute-done((bf16[1,128,12,64]{1,3,2,0:T(8,128)(2,1)S(1)}, bf16[1,128,12,64]{1,3,2,0:T(8,128)(2,1)S(1)}, u32[]{:S(2)}, u32[]{:S(2)}) %collective-permute-start.5) | collective-permute-done | bytes 196640 | tf_op jit(solution)/shard_map/while/body/eval_jaxpr/ppermute | solution.py:17
  317.9 8.4 %multiply_convert_fusion = (bf16[128,3072]{1,0:T(8,128)(2,1)S(1)}, f32[128,3072]{1,0:T(8,128)}, f32[128,3072]{1,0:T(8,128)}) fusion(f32[3072]{0:T(1024)S(1)} %copy-done.22, bf16[768,3072]{1,0:T(8,128)(2,1)} %all-gather.9.cloned.1.call-done, bf16[1,128,768]{2,1,0:T(8,128)(2,1)S(1)} %copy-done, f32[768]{0:T(1024)S(1)} %copy-done.12, f32[768]{0:T(1024)S(1)} %copy-done.9, ...), kind=kOutput, calls=%fused_computation.94 | convolution fusion | flops 630521856 | bytes 8866816 | tf_op jit(solution)/shard_map/dot_general | solution.py:142
  326.3 5.0 fusion.129
  338.8 4.7 fusion.131
  345.1 35.6 %reduce-scatter.5.cloned.1.call-done = bf16[192,2304]{1,0:T(8,128)(2,1)} async-done(((bf16[768,2304]{1,0:T(8,128)(2,1)}), bf16[192,2304]{1,0:T(8,128)(2,1)}) %reduce-scatter.5.cloned.1.call-update) | async-done | bytes 884752 | tf_op jit(solution)/shard_map/reduce_scatter | solution.py:270
  380.7 60.0 %reduce-scatter.9.cloned.1.call-done = bf16[192,3072]{1,0:T(8,128)(2,1)} async-done(((bf16[768,3072]{1,0:T(8,128)(2,1)}), bf16[192,3072]{1,0:T(8,128)(2,1)}) %reduce-scatter.9.cloned.1.call-update) | async-done | bytes 1179664 | tf_op jit(solution)/shard_map/reduce_scatter | solution.py:276
  440.7 60.0 %reduce-scatter.11.cloned.1.call-done = bf16[768,768]{1,0:T(8,128)(2,1)} async-done(((bf16[3072,768]{1,0:T(8,128)(2,1)}), bf16[768,768]{1,0:T(8,128)(2,1)}) %reduce-scatter.11.cloned.1.call-update) | async-done | bytes 1179664 | tf_op jit(solution)/shard_map/reduce_scatter | solution.py:279
  501.8 29.7 %all-reduce.6 = (bf16[768]{0:T(1024)(128)(2,1)S(1)}, bf16[768]{0:T(1024)(128)(2,1)S(1)}, bf16[768]{0:T(1024)(128)(2,1)S(1)}, bf16[768]{0:T(1024)(128)(2,1)S(1)},...) all-reduce(bf16[768]{0:T(1024)(128)(2,1)S(1)} %get-tuple-element.78, ...), channel_id=1, replica_groups=mesh['shard'=4,'ctx'=8] {'ctx'}, use_global_device_ids=true, to_apply=%region_28.29 | all-reduce | flops 8448 | bytes 33792 | tf_op jit(solution)/shard_map/psum | solution.py:262
  531.4 15.3 %all-reduce.8 = (bf16[768]{0:T(1024)(128)(2,1)S(1)}, bf16[768]{0:T(1024)(128)(2,1)S(1)}, bf16[768]{0:T(1024)(128)(2,1)S(1)}, bf16[768]{0:T(1024)(128)(2,1)S(1)},...) all-reduce(bf16[768]{0:T(1024)(128)(2,1)S(1)} %get-tuple-element.84, ...), channel_id=1, replica_groups=mesh['shard'=4,'ctx'=8] {'shard'}, use_global_device_ids=true, to_apply=%region_29.30 | all-reduce | flops 8448 | bytes 33792 | tf_op jit(solution)/shard_map/psum | solution.py:284
  555.7 32.2 %all-reduce.11.cloned.1.call-done = (bf16[192,2304]{1,0:T(8,128)(2,1)}, bf16[192,768]{1,0:T(8,128)(2,1)}, bf16[192,3072]{1,0:T(8,128)(2,1)}, bf16[768,768]{1,0:T(8,128)(2,1)}) async-done(((bf16[192,2304]{1,0:T(8,128)(2,1)}, bf16[192,768]{1,0:T(8,128)(2,1)}, bf16[192,3072]{1,0:T(8,128)(2,1)}, bf16[768,768]{1,0:T(8,128)(2,1)}), (bf16[192,2304]{1,0:T(8,128)(2,1)}, bf16[192,768]{1,0:T(8,128)(2,1)}, ...) | async-done | bytes 3538960 | tf_op jit(solution)/shard_map/psum | solution.py:258
  (338 shorter events, 197.3 us)
Async XLA Ops:
  7.2 33.0 %all-gather.7.cloned.1.call-start = ((), (), s32[]{:S(2)}) async-start(), calls=%async_computation.5 | async-start | bytes 1474560 | tf_op jit(solution)/shard_map/all_gather | solution.py:76
  7.9 81.2 %all-gather.5.cloned.1.call-start = ((), (), s32[]{:S(2)}) async-start(), calls=%async_computation.4 | async-start | bytes 4423680 | tf_op jit(solution)/shard_map/all_gather | solution.py:75
  8.7 308.8 %all-gather.9.cloned.1.call-start = ((), (), s32[]{:S(2)}) async-start(), calls=%async_computation.6 | async-start | bytes 5898240 | tf_op jit(solution)/shard_map/all_gather | solution.py:77
  9.5 316.8 %all-gather.11.cloned.1.call-start = ((), (), s32[]{:S(2)}) async-start(), calls=%async_computation.7 | async-start | bytes 5898240 | tf_op jit(solution)/shard_map/all_gather | solution.py:78
  10.0 335.0 %reduce-scatter.7.cloned.1.call-start = ((), (), s32[]{:S(2)}) async-start(), calls=%async_computation.9 | async-start | bytes 1474560 | tf_op jit(solution)/shard_map/reduce_scatter | solution.py:273
  94.8 9.0 %collective-permute-start = (bf16[1,128,12,64]{1,3,2,0:T(8,128)(2,1)S(1)}, bf16[1,128,12,64]{1,3,2,0:T(8,128)(2,1)S(1)}, u32[]{:S(2)}, u32[]{:S(2)}) collective-permute-start(bf16[1,128,12,64]{1,3,2,0:T(8,128)(2,1)S(1)} %get-tuple-element.1113), channel_id=1, source_target_pairs={{0,1},{1,2},{2,3},{3,4},{4,5},{5,6},{6,7},{7,0},{8,9},{9,10},{10,1... | collective-permute-start | bytes 589832 | tf_op jit(solution)/shard_map/while/body/eval_jaxpr/ppermute | solution.py:17
  106.8 9.0 %collective-permute-start = (bf16[1,128,12,64]{1,3,2,0:T(8,128)(2,1)S(1)}, bf16[1,128,12,64]{1,3,2,0:T(8,128)(2,1)S(1)}, u32[]{:S(2)}, u32[]{:S(2)}) collective-permute-start(bf16[1,128,12,64]{1,3,2,0:T(8,128)(2,1)S(1)} %get-tuple-element.1113), channel_id=1, source_target_pairs={{0,1},{1,2},{2,3},{3,4},{4,5},{5,6},{6,7},{7,0},{8,9},{9,10},{10,1... | collective-permute-start | bytes 589832 | tf_op jit(solution)/shard_map/while/body/eval_jaxpr/ppermute | solution.py:17
  118.8 9.0 %collective-permute-start = (bf16[1,128,12,64]{1,3,2,0:T(8,128)(2,1)S(1)}, bf16[1,128,12,64]{1,3,2,0:T(8,128)(2,1)S(1)}, u32[]{:S(2)}, u32[]{:S(2)}) collective-permute-start(bf16[1,128,12,64]{1,3,2,0:T(8,128)(2,1)S(1)} %get-tuple-element.1113), channel_id=1, source_target_pairs={{0,1},{1,2},{2,3},{3,4},{4,5},{5,6},{6,7},{7,0},{8,9},{9,10},{10,1... | collective-permute-start | bytes 589832 | tf_op jit(solution)/shard_map/while/body/eval_jaxpr/ppermute | solution.py:17
  127.9 9.0 %collective-permute-start = (bf16[1,128,12,64]{1,3,2,0:T(8,128)(2,1)S(1)}, bf16[1,128,12,64]{1,3,2,0:T(8,128)(2,1)S(1)}, u32[]{:S(2)}, u32[]{:S(2)}) collective-permute-start(bf16[1,128,12,64]{1,3,2,0:T(8,128)(2,1)S(1)} %get-tuple-element.1113), channel_id=1, source_target_pairs={{0,1},{1,2},{2,3},{3,4},{4,5},{5,6},{6,7},{7,0},{8,9},{9,10},{10,1... | collective-permute-start | bytes 589832 | tf_op jit(solution)/shard_map/while/body/eval_jaxpr/ppermute | solution.py:17
  137.0 9.0 %collective-permute-start = (bf16[1,128,12,64]{1,3,2,0:T(8,128)(2,1)S(1)}, bf16[1,128,12,64]{1,3,2,0:T(8,128)(2,1)S(1)}, u32[]{:S(2)}, u32[]{:S(2)}) collective-permute-start(bf16[1,128,12,64]{1,3,2,0:T(8,128)(2,1)S(1)} %get-tuple-element.1113), channel_id=1, source_target_pairs={{0,1},{1,2},{2,3},{3,4},{4,5},{5,6},{6,7},{7,0},{8,9},{9,10},{10,1... | collective-permute-start | bytes 589832 | tf_op jit(solution)/shard_map/while/body/eval_jaxpr/ppermute | solution.py:17
  146.2 9.0 %collective-permute-start = (bf16[1,128,12,64]{1,3,2,0:T(8,128)(2,1)S(1)}, bf16[1,128,12,64]{1,3,2,0:T(8,128)(2,1)S(1)}, u32[]{:S(2)}, u32[]{:S(2)}) collective-permute-start(bf16[1,128,12,64]{1,3,2,0:T(8,128)(2,1)S(1)} %get-tuple-element.1113), channel_id=1, source_target_pairs={{0,1},{1,2},{2,3},{3,4},{4,5},{5,6},{6,7},{7,0},{8,9},{9,10},{10,1... | collective-permute-start | bytes 589832 | tf_op jit(solution)/shard_map/while/body/eval_jaxpr/ppermute | solution.py:17
  158.2 9.0 %collective-permute-start = (bf16[1,128,12,64]{1,3,2,0:T(8,128)(2,1)S(1)}, bf16[1,128,12,64]{1,3,2,0:T(8,128)(2,1)S(1)}, u32[]{:S(2)}, u32[]{:S(2)}) collective-permute-start(bf16[1,128,12,64]{1,3,2,0:T(8,128)(2,1)S(1)} %get-tuple-element.1113), channel_id=1, source_target_pairs={{0,1},{1,2},{2,3},{3,4},{4,5},{5,6},{6,7},{7,0},{8,9},{9,10},{10,1... | collective-permute-start | bytes 589832 | tf_op jit(solution)/shard_map/while/body/eval_jaxpr/ppermute | solution.py:17
  168.8 211.9 %reduce-scatter.5.cloned.1.call-start = ((), (), s32[]{:S(2)}) async-start(), calls=%async_computation.8 | async-start | bytes 4423680 | tf_op jit(solution)/shard_map/reduce_scatter | solution.py:270
  171.5 8.9 %collective-permute-start.6 = (bf16[1,128,12,64]{1,3,2,0:T(8,128)(2,1)S(1)}, bf16[1,128,12,64]{1,3,2,0:T(8,128)(2,1)S(1)}, u32[]{:S(2)}, u32[]{:S(2)}) collective-permute-start(bf16[1,128,12,64]{1,3,2,0:T(8,128)(2,1)S(1)} %convert_element_type.289), channel_id=1, source_target_pairs={{0,1},{1,2},{2,3},{3,4},{4,5},{5,6},{6,7},{7,0},{8,9},{9,10},{10,1... | collective-permute-start | bytes 589832 | tf_op jit(solution)/shard_map/ppermute | solution.py:17
  180.6 9.0 %collective-permute-start.2 = (bf16[1,128,12,64]{1,3,2,0:T(8,128)(2,1)S(1)}, bf16[1,128,12,64]{1,3,2,0:T(8,128)(2,1)S(1)}, u32[]{:S(2)}, u32[]{:S(2)}) collective-permute-start(bf16[1,128,12,64]{1,3,2,0:T(8,128)(2,1)S(1)} %get-tuple-element.1171), channel_id=1, source_target_pairs={{0,1},{1,2},{2,3},{3,4},{4,5},{5,6},{6,7},{7,0},{8,9},{9,10},{10,1... | collective-permute-start | bytes 589832 | tf_op jit(solution)/shard_map/while/body/eval_jaxpr/ppermute | solution.py:17
  200.6 9.0 %collective-permute-start.2 = (bf16[1,128,12,64]{1,3,2,0:T(8,128)(2,1)S(1)}, bf16[1,128,12,64]{1,3,2,0:T(8,128)(2,1)S(1)}, u32[]{:S(2)}, u32[]{:S(2)}) collective-permute-start(bf16[1,128,12,64]{1,3,2,0:T(8,128)(2,1)S(1)} %get-tuple-element.1171), channel_id=1, source_target_pairs={{0,1},{1,2},{2,3},{3,4},{4,5},{5,6},{6,7},{7,0},{8,9},{9,10},{10,1... | collective-permute-start | bytes 589832 | tf_op jit(solution)/shard_map/while/body/eval_jaxpr/ppermute | solution.py:17
  220.7 9.0 %collective-permute-start.2 = (bf16[1,128,12,64]{1,3,2,0:T(8,128)(2,1)S(1)}, bf16[1,128,12,64]{1,3,2,0:T(8,128)(2,1)S(1)}, u32[]{:S(2)}, u32[]{:S(2)}) collective-permute-start(bf16[1,128,12,64]{1,3,2,0:T(8,128)(2,1)S(1)} %get-tuple-element.1171), channel_id=1, source_target_pairs={{0,1},{1,2},{2,3},{3,4},{4,5},{5,6},{6,7},{7,0},{8,9},{9,10},{10,1... | collective-permute-start | bytes 589832 | tf_op jit(solution)/shard_map/while/body/eval_jaxpr/ppermute | solution.py:17
  238.8 9.0 %collective-permute-start.2 = (bf16[1,128,12,64]{1,3,2,0:T(8,128)(2,1)S(1)}, bf16[1,128,12,64]{1,3,2,0:T(8,128)(2,1)S(1)}, u32[]{:S(2)}, u32[]{:S(2)}) collective-permute-start(bf16[1,128,12,64]{1,3,2,0:T(8,128)(2,1)S(1)} %get-tuple-element.1171), channel_id=1, source_target_pairs={{0,1},{1,2},{2,3},{3,4},{4,5},{5,6},{6,7},{7,0},{8,9},{9,10},{10,1... | collective-permute-start | bytes 589832 | tf_op jit(solution)/shard_map/while/body/eval_jaxpr/ppermute | solution.py:17
  257.0 9.0 %collective-permute-start.2 = (bf16[1,128,12,64]{1,3,2,0:T(8,128)(2,1)S(1)}, bf16[1,128,12,64]{1,3,2,0:T(8,128)(2,1)S(1)}, u32[]{:S(2)}, u32[]{:S(2)}) collective-permute-start(bf16[1,128,12,64]{1,3,2,0:T(8,128)(2,1)S(1)} %get-tuple-element.1171), channel_id=1, source_target_pairs={{0,1},{1,2},{2,3},{3,4},{4,5},{5,6},{6,7},{7,0},{8,9},{9,10},{10,1... | collective-permute-start | bytes 589832 | tf_op jit(solution)/shard_map/while/body/eval_jaxpr/ppermute | solution.py:17
  275.2 9.0 %collective-permute-start.2 = (bf16[1,128,12,64]{1,3,2,0:T(8,128)(2,1)S(1)}, bf16[1,128,12,64]{1,3,2,0:T(8,128)(2,1)S(1)}, u32[]{:S(2)}, u32[]{:S(2)}) collective-permute-start(bf16[1,128,12,64]{1,3,2,0:T(8,128)(2,1)S(1)} %get-tuple-element.1171), channel_id=1, source_target_pairs={{0,1},{1,2},{2,3},{3,4},{4,5},{5,6},{6,7},{7,0},{8,9},{9,10},{10,1... | collective-permute-start | bytes 589832 | tf_op jit(solution)/shard_map/while/body/eval_jaxpr/ppermute | solution.py:17
  295.3 9.0 %collective-permute-start.2 = (bf16[1,128,12,64]{1,3,2,0:T(8,128)(2,1)S(1)}, bf16[1,128,12,64]{1,3,2,0:T(8,128)(2,1)S(1)}, u32[]{:S(2)}, u32[]{:S(2)}) collective-permute-start(bf16[1,128,12,64]{1,3,2,0:T(8,128)(2,1)S(1)} %get-tuple-element.1171), channel_id=1, source_target_pairs={{0,1},{1,2},{2,3},{3,4},{4,5},{5,6},{6,7},{7,0},{8,9},{9,10},{10,1... | collective-permute-start | bytes 589832 | tf_op jit(solution)/shard_map/while/body/eval_jaxpr/ppermute | solution.py:17
  317.2 123.5 %reduce-scatter.9.cloned.1.call-start = ((), (), s32[]{:S(2)}) async-start(), calls=%async_computation.10 | async-start | bytes 5898240 | tf_op jit(solution)/shard_map/reduce_scatter | solution.py:276
  335.1 165.6 %reduce-scatter.11.cloned.1.call-start = ((), (), s32[]{:S(2)}) async-start(), calls=%async_computation.11 | async-start | bytes 5898240 | tf_op jit(solution)/shard_map/reduce_scatter | solution.py:279
  338.7 249.2 %all-reduce.11.cloned.1.call-start = ((), (), s32[]{:S(2)}) async-start(), calls=%async_computation.12 | async-start | bytes 7077888 | tf_op jit(solution)/shard_map/psum | solution.py:258
  (52 other events, 815.8 us)
Sparse Core Ops, SparseCore 0:
  9.8 30.2 all-gather.6
  42.0 47.1 all-gather.4
  91.0 56.9 all-gather.8
  149.7 56.9 all-gather.10
  210.0 28.7 reduce-scatter.6
  317.3 63.3 reduce-scatter.4
  383.7 56.9 reduce-scatter.8
  443.7 56.9 reduce-scatter.10
  503.3 84.5 all-reduce.10
where the time goes:
time: 604 us; the launch traced here: 602 us
  waiting for transfers between devices  408 us (68%)
  blocking collectives  59 us (10%)
  matrix products  49.6 us (8%)
  other arithmetic  40.6 us (7%)
  loops' own time  19.8 us (3%)
  between operations  15.6 us (3%)
    ppermute x44, waiting for transfers between devices, shifted(): lax.ppermute(shard, axis, [(i, (i + by) % count) for i in range(count)])  157 us
    reduce_scatter x1, waiting for transfers between devices, on_device(): lax.psum_scatter(summed[2].astype(jnp.bfloat16), 'shard', scatter_dimensi...  60 us
    reduce_scatter x1, waiting for transfers between devices, on_device(): lax.psum_scatter(summed[3].astype(jnp.bfloat16), 'shard', scatter_dimensi...  60 us
    all_gather x1, waiting for transfers between devices, on_device(): lax.all_gather(w_qkv, 'shard', axis=0, tiled=True)  47 us
    reduce_scatter x1, waiting for transfers between devices, on_device(): lax.psum_scatter(summed[0].astype(jnp.bfloat16), 'shard', scatter_dimensi...  35.6 us
    psum x1, waiting for transfers between devices, on_device(): lax.psum(grad_qkv.astype(jnp.bfloat16), 'ctx').astype(jnp.float32)  32.2 us
    psum x1, blocking collectives, on_device(): lax.psum(grad_gain_one.astype(jnp.bfloat16), 'ctx').astype(jnp.float32)  29.7 us
    psum x1, blocking collectives, on_device(): lax.psum(summed[4].astype(jnp.bfloat16), 'shard').astype(jnp.float32)  15.3 us
  transfers between devices with their start and end apart: 53, of which 50 were waited for; matrix products, arithmetic and copies ran while one was open for 14% of the time, Pallas kernels for 0%

commit v1 on v0

--- a/solution.py
+++ b/solution.py
@@ -1,6 +1,9 @@
 import jax
 import jax.numpy as jnp
+import numpy as np
 from jax import lax
+from jax.experimental import pallas as pl
+from jax.experimental.pallas import tpu as pltpu
 from jax.sharding import PartitionSpec as P
 
 HEADS = 12
@@ -51,7 +54,649 @@
     return jax.nn.gelu(field_in, approximate=False)
 
 
-def on_device(
+MESH = pl.DeviceIdType.MESH
+LOW = jnp.bfloat16
+FULL = jnp.float32
+ROWS_CONTRACT = (((0,), (0,)), ((), ()))
+COLS_CONTRACT = (((1,), (1,)), ((), ()))
+INV_ROOT_TWO = 0.7071067811865476
+INV_ROOT_TWO_PI = 0.3989422804014327
+LINE_LAG = 3
+
+
+def dot(lhs, rhs, dims=(((1,), (0,)), ((), ()))):
+    return lax.dot_general(lhs, rhs, dims, preferred_element_type=FULL)
+
+
+def flip(index, bits):
+    for power in (1, 2, 4, 8):
+        if bits & power:
+            index = index + power - 2 * power * lax.rem(lax.div(index, power), 2)
+    return index
+
+
+def at16(value):
+    return pl.multiple_of(value, 16)
+
+
+def at128(value):
+    return pl.multiple_of(value, 128)
+
+
+def rotary_constants(blocks, block_len):
+    lane = np.arange(128) % HEAD_DIM
+    half = ROTARY // 2
+    turning = lane < ROTARY
+    freq = np.where(turning, 10000.0 ** (-(lane % half) * (2.0 / ROTARY)), 0.0)
+    sign = np.where(lane < half, -1.0, 1.0) * turning
+    offset = np.arange(block_len)[:, None] * freq
+    start = (np.arange(blocks) * block_len)[:, None] * freq
+    parts = (np.cos(offset), np.sin(offset) * sign, np.cos(start), np.sin(start) * sign)
+    return np.concatenate(parts).astype(np.float32)
+
+
+def fused_body(
+    x_ref,
+    pos_ref,
+    gain1_ref,
+    bias1_ref,
+    gain2_ref,
+    bias2_ref,
+    qkvb_ref,
+    upb_ref,
+    rot_ref,
+    cot_hbm,
+    wsel_hbm,
+    wup_hbm,
+    wout_hbm,
+    wdn_hbm,
+    y_ref,
+    dx_ref,
+    fin_ref,
+    qkvfin_ref,
+    small_ref,
+    wq,
+    wup,
+    wout,
+    wdn,
+    n1,
+    n2,
+    cot,
+    pos_tx,
+    pos_rx,
+    pos_sm,
+    qkv,
+    q_s,
+    k_s,
+    v_s,
+    do_tx,
+    do_rx,
+    do_s,
+    o_s,
+    dq_s,
+    dk_s,
+    dv_s,
+    gp_s,
+    gp_e,
+    o_tx,
+    o_rx,
+    attn_low,
+    a1_p,
+    a1_d2d,
+    a1_c,
+    a1_rx,
+    gq_tx,
+    gq_rx,
+    gq_sum,
+    out_acc,
+    a2_acc,
+    out_tx,
+    out_rx,
+    a2_tx,
+    a2_rx,
+    gd16,
+    gd_rx,
+    gu16,
+    gu_rx,
+    gu_tx,
+    go16,
+    go_rx,
+    go_tx,
+    go_x,
+    line_own,
+    line_rx,
+    line_near,
+    line_far,
+    small_a,
+    small_rx,
+    small_b,
+    small_bx,
+    ssem,
+    rsem,
+    lsem,
+):
+    shards = lax.axis_size("shard")
+    ctxs = lax.axis_size("ctx")
+    s = lax.axis_index("shard")
+    i = lax.axis_index("ctx")
+    c = lax.rem(i, 2)
+    z = lax.div(i, 2)
+    other = 1 - c
+    planes = range(1, shards)
+    mates = range(1, ctxs)
+    even = range(2, ctxs, 2)
+    block = x_ref.shape[0]
+    width = x_ref.shape[1]
+    rows = width // shards
+    half_rows = rows // 2
+    sent = []
+    used = [0]
+
+    def channels(count):
+        first = used[0]
+        used[0] += count
+        return first
+
+    def remote(k, src, dst, device):
+        return pltpu.make_async_remote_copy(
+            src_ref=src,
+            dst_ref=dst,
+            send_sem=ssem.at[k],
+            recv_sem=rsem.at[k],
+            device_id=device,
+            device_id_type=MESH,
+        )
+
+    def send(k, src, dst, **device):
+        copy = remote(k, src, dst, device)
+        copy.start()
+        sent.append(copy)
+
+    def arrived(k, dst):
+        remote(k, dst, dst, {"ctx": flip(i, 1)}).wait_recv()
+
+    def plane(d):
+        return flip(s, d)
+
+    def mate(e):
+        return flip(i, e)
+
+    loads = []
+
+    def load(k, src, dst):
+        copy = pltpu.make_async_copy(src, dst, lsem.at[k])
+        copy.start()
+        loads.append(copy)
+
+    my_rows = pl.ds(at16(s * rows), rows)
+    load(0, cot_hbm, cot.at[pl.ds(0, block)])
+    load(1, wsel_hbm, wq.at[my_rows])
+    load(2, wout_hbm, wout.at[my_rows])
+    load(3, wup_hbm.at[:, pl.ds(at128(s * width), width)], wup.at[my_rows])
+    load(4, wdn_hbm, wdn)
+
+    barrier = pltpu.get_barrier_semaphore()
+    for d in planes:
+        pl.semaphore_signal(barrier, inc=1, device_id={"shard": plane(d)}, device_id_type=MESH)
+    for e in mates:
+        pl.semaphore_signal(barrier, inc=1, device_id={"ctx": mate(e)}, device_id_type=MESH)
+    pl.semaphore_wait(barrier, shards + ctxs - 2)
+
+    K_WQ = channels(shards)
+    K_WO = channels(shards)
+    K_WO2 = channels(shards)
+    K_WU = channels(shards)
+    K_WU2 = channels(shards)
+    K_COT = channels(shards)
+    K_N2 = channels(shards)
+    K_POS = channels(ctxs)
+    K_N1 = channels(ctxs)
+    for d in planes:
+        send(K_WQ + d, wsel_hbm, wq.at[my_rows], shard=plane(d))
+    my_half = pl.ds(at16(s * rows + c * half_rows), half_rows)
+    for d in planes:
+        send(
+            K_WO + d, wout_hbm.at[pl.ds(at16(c * half_rows), half_rows)], wout.at[my_half],
+            shard=plane(d),
+        )
+    pos_tx[...] = jnp.broadcast_to(pos_ref[...], pos_tx.shape)
+    x = x_ref[...].astype(FULL)
+    mean = jnp.mean(x, axis=-1, keepdims=True)
+    centered = x - mean
+    r = lax.rsqrt(jnp.mean(centered * centered, axis=-1, keepdims=True) + EPSILON)
+    normal = centered * r
+    n1[pl.ds(0, block)] = (normal * gain1_ref[...] + bias1_ref[...]).astype(LOW)
+    n2[pl.ds(0, block)] = (normal * gain2_ref[...] + bias2_ref[...]).astype(LOW)
+    pos_rx[0] = pos_tx[...]
+    for e in mates:
+        send(K_POS + e, pos_tx, pos_rx.at[e], ctx=mate(e))
+    for e in (1, *even):
+        send(K_N1 + e, n1.at[pl.ds(0, block)], n1.at[pl.ds(block * e, block)], ctx=mate(e))
+    for d in planes:
+        send(
+            K_WU + d,
+            wup_hbm.at[
+                pl.ds(at16(c * half_rows), half_rows), pl.ds(at128(plane(d) * width), width)
+            ],
+            wup.at[my_half],
+            shard=plane(d),
+        )
+    for d in planes:
+        send(K_N2 + d, n2.at[pl.ds(0, block)], n2.at[pl.ds(block * d, block)], shard=plane(d))
+    for d in planes:
+        send(K_COT + d, cot_hbm, cot.at[pl.ds(block * d, block)], shard=plane(d))
+    for copy in loads:
+        copy.wait()
+
+    def rows_of(d, core):
+        return pl.ds(at16(plane(d) * rows + core * half_rows), half_rows)
+
+    for d in planes:
+        arrived(K_WO + d, wout.at[rows_of(d, c)])
+        send(K_WO2 + d, wout.at[rows_of(d, c)], wout.at[rows_of(d, c)], ctx=mate(1))
+    for d in planes:
+        arrived(K_WO2 + d, wout.at[rows_of(d, other)])
+
+    lane = lax.broadcasted_iota(jnp.int32, (block, 128), 1)
+    low_lanes = lane < HEAD_DIM
+    K_DO = channels(ctxs)
+    grad_attn = dot(cot[pl.ds(0, block)], wout[...], COLS_CONTRACT)
+    for w in range(width // 384):
+        t0, t1, t2 = (grad_attn[:, 384 * w + 128 * t : 384 * w + 128 * (t + 1)] for t in range(3))
+        turned = pltpu.roll(t1, HEAD_DIM, 1)
+        do_tx[4 * w] = t0.astype(LOW)
+        do_tx[4 * w + 1] = jnp.where(low_lanes, pltpu.roll(t0, HEAD_DIM, 1), turned).astype(LOW)
+        do_tx[4 * w + 2] = jnp.where(low_lanes, turned, pltpu.roll(t2, HEAD_DIM, 1)).astype(LOW)
+        do_tx[4 * w + 3] = t2.astype(LOW)
+    for e in mates:
+        send(K_DO + e, do_tx.at[mate(e)], do_rx.at[e], ctx=mate(e))
+    do_rx[0] = do_tx[i]
+
+    for e in even:
+        arrived(K_N1 + e, n1.at[pl.ds(block * e, block)])
+        send(K_N1 + e + 1, n1.at[pl.ds(block * e, block)], n1.at[pl.ds(block * (e + 1), block)], ctx=mate(1))
+    arrived(K_N1 + 1, n1.at[pl.ds(block, block)])
+    for e in even:
+        arrived(K_N1 + e + 1, n1.at[pl.ds(block * (e + 1), block)])
+    for d in planes:
+        arrived(K_WQ + d, wq.at[pl.ds(at16(plane(d) * rows), rows)])
+
+    @pl.loop(0, ctxs // 2)
+    def _(m):
+        here = pl.ds(at128(m * 2 * block), 2 * block)
+        qkv[pl.ds(2 * m, 2)] = dot(n1[here], wq[...]).reshape(2, block, 384)
+
+    for e in mates:
+        arrived(K_POS + e, pos_rx.at[e])
+    to_scalar = pltpu.make_async_copy(pos_rx, pos_sm, lsem.at[5])
+    to_scalar.start()
+    to_scalar.wait()
+    rank = [lax.div(pos_sm[e, 0, 0], block) for e in range(ctxs)]
+    place = []
+    for g in range(ctxs):
+        found = jnp.int32(0)
+        for e in range(1, ctxs):
+            found = found + e * (rank[e] == g).astype(jnp.int32)
+        place.append(lax.rem(found, ctxs))
+
+    leads = lax.rem(lane, HEAD_DIM) < ROTARY // 2
+
+    def across(field):
+        return jnp.where(
+            leads,
+            pltpu.roll(field, 128 - ROTARY // 2, 1),
+            pltpu.roll(field, ROTARY // 2, 1),
+        )
+
+    def tables(g):
+        off_cos, off_sin = rot_ref[pl.ds(0, block)], rot_ref[pl.ds(block, block)]
+        start_cos = rot_ref[pl.ds(2 * block + g, 1)]
+        start_sin = rot_ref[pl.ds(2 * block + ctxs + g, 1)]
+        cosine = start_cos * off_cos - start_sin * off_sin
+        sine = start_sin * off_cos + start_cos * off_sin
+        return cosine, sine
+
+    for e in mates:
+        arrived(K_DO + e, do_rx.at[e])
+    for g in range(ctxs):
+        here = pl.ds(block * g, block)
+        field = qkv[place[g]] + qkvb_ref[...]
+        cosine, sine = tables(g)
+        q_raw, k_raw = field[:, :128], field[:, 128:256]
+        turned_q = (q_raw * cosine + across(q_raw) * sine).astype(LOW)
+        q_s[here] = turned_q * jnp.asarray(HEAD_DIM**-0.5, LOW)
+        k_s[here] = (k_raw * cosine + across(k_raw) * sine).astype(LOW)
+        v_s[here] = field[:, 256:].astype(LOW)
+        do_s[here] = do_rx[place[g]]
+
+    for d in planes:
+        arrived(K_WU + d, wup.at[rows_of(d, c)])
+        send(K_WU2 + d, wup.at[rows_of(d, c)], wup.at[rows_of(d, c)], ctx=mate(1))
+
+    o_s[...] = jnp.zeros_like(o_s)
+    dq_s[...] = jnp.zeros_like(dq_s)
+    dk_s[...] = jnp.zeros_like(dk_s)
+    dv_s[...] = jnp.zeros_like(dv_s)
+
+    @pl.loop(0, 2)
+    def _(h):
+        mine = lax.div(lane, HEAD_DIM) == h
+        for g in range(ctxs):
+            share = 0 if g % 4 in (0, 3) else 1
+
+            @pl.when((h == c) | (c == share))
+            def _():
+                here = pl.ds(block * g, block)
+                upto = pl.ds(0, block * (g + 1))
+                span = block * (g + 1)
+                zero = jnp.zeros((block, 128), LOW)
+                q_h = jnp.where(mine, q_s[here], zero)
+                do_h = jnp.where(mine, do_s[here], zero)
+                scores = dot(q_h, k_s[upto], COLS_CONTRACT)
+                token = lax.broadcasted_iota(jnp.int32, (block, span), 0) + block * g
+                key = lax.broadcasted_iota(jnp.int32, (block, span), 1)
+                masked = jnp.where(key <= token, scores, NEGATIVE)
+                top = jnp.max(masked, axis=-1, keepdims=True)
+                weight = jnp.exp(masked - top)
+                probability = weight * (1.0 / jnp.sum(weight, axis=-1, keepdims=True))
+                prob_low = probability.astype(LOW)
+                attended = jnp.where(mine, dot(prob_low, v_s[upto]), 0.0)
+                o_s[g] += attended
+                grad_prob = dot(do_h, v_s[upto], COLS_CONTRACT)
+                row_delta = jnp.sum(do_h.astype(FULL) * attended, axis=-1, keepdims=True)
+                grad_score = (probability * (grad_prob - row_delta)).astype(LOW)
+                dq_s[here] += jnp.where(mine, dot(grad_score, k_s[upto]), 0.0)
+                dk_s[upto] += dot(grad_score, q_h, ROWS_CONTRACT)
+                dv_s[upto] += dot(prob_low, do_h, ROWS_CONTRACT)
+
+    K_O = channels(ctxs)
+    for e in range(ctxs):
+        o_tx[e] = o_s[rank[e]].astype(LOW)
+    for e in mates:
+        send(K_O + e, o_tx.at[e], o_rx.at[e], ctx=mate(e))
+    o_rx[0] = o_tx[0]
+
+    bias_sum = jnp.zeros((1, 384), FULL)
+    for g in range(ctxs):
+        here = pl.ds(block * g, block)
+        cosine, sine = tables(g)
+        dq = dq_s[here] * (HEAD_DIM**-0.5)
+        dk = dk_s[here]
+        parts = (dq * cosine - across(dq) * sine, dk * cosine - across(dk) * sine, dv_s[here])
+        part = jnp.concatenate(parts, axis=1).astype(LOW)
+        gp_s[g] = part
+        bias_sum = bias_sum + jnp.sum(part.astype(FULL), axis=0, keepdims=True)
+    for e in range(ctxs):
+        gp_e[pl.ds(block * e, block)] = gp_s[rank[e]]
+
+    @pl.loop(0, ctxs * block // 256)
+    def _(m):
+        here = pl.ds(at128(m * 256), 256)
+        a1_p[here] = dot(gp_e[here], wq[...], COLS_CONTRACT).astype(LOW)
+
+    K_A1 = channels(ctxs)
+    K_A1D = channels(ctxs)
+    for k in range(ctxs // 2):
+        send(K_A1D + k, a1_p.at[pl.ds(block * (2 * k + 1), block)], a1_d2d.at[k], ctx=mate(1))
+
+    @pl.loop(0, width // 256)
+    def _(m):
+        here = pl.ds(at128(m * 256), 256)
+        gq_tx[here] = dot(n1[:, here], gp_e[...], ROWS_CONTRACT).astype(LOW)
+
+    K_GQ = channels(shards)
+    for d in planes:
+        send(K_GQ + d, gq_tx.at[pl.ds(at16(plane(d) * rows), rows)], gq_rx.at[d], shard=plane(d))
+    for k in range(ctxs // 2):
+        arrived(K_A1D + k, a1_d2d.at[k])
+        total = a1_p[pl.ds(block * 2 * k, block)].astype(FULL) + a1_d2d[k].astype(FULL)
+        a1_c[k] = total.astype(LOW)
+        if k:
+            send(K_A1 + k, a1_c.at[k], a1_rx.at[k], ctx=mate(2 * k))
+
+    for d in planes:
+        arrived(K_WU2 + d, wup.at[rows_of(d, other)])
+        arrived(K_N2 + d, n2.at[pl.ds(block * d, block)])
+        arrived(K_COT + d, cot.at[pl.ds(block * d, block)])
+    out_acc[...] = jnp.zeros_like(out_acc)
+    a2_acc[...] = jnp.zeros_like(a2_acc)
+
+    @pl.loop(0, width // 256)
+    def _(t):
+        units = pl.ds(at128(t * 256), 256)
+        bias = upb_ref[:, pl.ds(at128(s * width + t * 256), 256)]
+        pre = dot(n2[...], wup[:, units]) + bias
+        cdf = 0.5 * (1.0 + lax.erf(pre * INV_ROOT_TWO))
+        hidden = (pre * cdf).astype(LOW)
+        slope = cdf + pre * (jnp.exp(-0.5 * pre * pre) * INV_ROOT_TWO_PI)
+        grad_hidden = dot(cot[...], wdn[units], COLS_CONTRACT)
+        grad_pre = (grad_hidden * slope).astype(LOW)
+        small_a[4:5, units] = jnp.sum(grad_pre.astype(FULL), axis=0, keepdims=True)
+        out_acc[...] += dot(hidden, wdn[units])
+        a2_acc[...] += dot(grad_pre, wup[:, units], COLS_CONTRACT)
+        gd16[units] = dot(hidden, cot[...], ROWS_CONTRACT).astype(LOW)
+        gu16[:, units] = dot(n2[...], grad_pre, ROWS_CONTRACT).astype(LOW)
+
+    K_GD = channels(1)
+    K_GU = channels(shards)
+    K_GUX = channels(shards)
+    K_OUT = channels(shards)
+    K_A2 = channels(shards)
+    half_width = width // 2
+    send(K_GD, gd16.at[pl.ds(at16(other * half_width), half_width)], gd_rx, ctx=mate(1))
+    for d in range(shards):
+        send(K_GU + d, gu16.at[rows_of(d, other)], gu_rx.at[d], ctx=mate(1))
+    for d in planes:
+        out_tx[d] = out_acc[pl.ds(block * d, block)].astype(LOW)
+        a2_tx[d] = a2_acc[pl.ds(block * d, block)].astype(LOW)
+
+    def up_rows(index):
+        return pl.ds(at16(half_width + index * half_rows), half_rows)
+
+    Z = ctxs // 2
+    is_end = (z == 0) | (z == Z - 1)
+    is_centre = (z == Z // 2 - 1) | (z == Z // 2)
+    inward = jnp.where(z < Z // 2, 2, -2)
+    to_inner = jnp.where(is_centre, 1, 0)
+    line_rows = half_width + rows * shards // 2 + half_rows
+    chunk = half_rows
+    chunks = line_rows // chunk
+    K_LINE = channels(2 * chunks)
+    K_FAR = channels(chunks)
+    K_FIN = channels(chunks)
+
+    def span_of(q):
+        return pl.ds(q * chunk, chunk)
+
+    def near_copy(q, src):
+        return pltpu.make_async_remote_copy(
+            src_ref=src.at[span_of(q)],
+            dst_ref=line_rx.at[to_inner, span_of(q)],
+            send_sem=ssem.at[K_LINE + q],
+            recv_sem=rsem.at[K_LINE + chunks * to_inner + q],
+            device_id={"ctx": i + inward},
+            device_id_type=MESH,
+        )
+
+    def far_copy(q):
+        return pltpu.make_async_remote_copy(
+            src_ref=line_far.at[span_of(q)],
+            dst_ref=line_rx.at[1, span_of(q)],
+            send_sem=ssem.at[K_FAR + q],
+            recv_sem=rsem.at[K_LINE + chunks + q],
+            device_id={"ctx": i - inward},
+            device_id_type=MESH,
+        )
+
+    def near(q):
+        @pl.when(is_end)
+        def _():
+            line_rx[0, span_of(q)] = jnp.zeros((chunk, width), LOW)
+            near_copy(q, line_own).start()
+
+        @pl.when(jnp.logical_not(is_end))
+        def _():
+            arrived(K_LINE + q, line_rx.at[0, span_of(q)])
+            line_near[span_of(q)] = (
+                line_rx[0, span_of(q)].astype(FULL) + line_own[span_of(q)].astype(FULL)
+            ).astype(LOW)
+            near_copy(q, line_near).start()
+
+    def far(q):
+        arrived(K_LINE + chunks + q, line_rx.at[1, span_of(q)])
+        beyond = line_rx[1, span_of(q)].astype(FULL) + line_own[span_of(q)].astype(FULL)
+
+        @pl.when(jnp.logical_not(is_end))
+        def _():
+            line_far[span_of(q)] = beyond.astype(LOW)
+            far_copy(q).start()
+
+        fin_ref[c, span_of(q)] = (beyond + line_rx[0, span_of(q)].astype(FULL)).astype(LOW)
+        send(K_FIN + q, fin_ref.at[c, span_of(q)], fin_ref.at[c, span_of(q)], ctx=mate(1))
+
+    for d in range(shards):
+        arrived(K_GU + d, gu_rx.at[d])
+        total = (gu16[rows_of(d, c)].astype(FULL) + gu_rx[d].astype(FULL)).astype(LOW)
+        if d:
+            gu_tx[d] = total
+            send(K_GUX + d, gu_tx.at[d], line_own.at[up_rows(s)], shard=plane(d))
+        else:
+            line_own[up_rows(s)] = total
+    for d in planes:
+        send(K_OUT + d, out_tx.at[d], out_rx.at[d], shard=plane(d))
+        send(K_A2 + d, a2_tx.at[d], a2_rx.at[d], shard=plane(d))
+    arrived(K_GD, gd_rx)
+    line_own[pl.ds(0, half_width)] = (
+        gd16[pl.ds(at16(c * half_width), half_width)].astype(FULL) + gd_rx[...].astype(FULL)
+    ).astype(LOW)
+    for q in range(4):
+        near(q)
+
+    for e in mates:
+        arrived(K_O + e, o_rx.at[e])
+    for w in range(width // 384):
+        p0, p1, p2, p3 = (o_rx[flip(i, 4 * w + t)].astype(FULL) for t in range(4))
+        r1, r2 = pltpu.roll(p1, HEAD_DIM, 1), pltpu.roll(p2, HEAD_DIM, 1)
+        base = 384 * w
+        attn_low[:, base : base + 128] = (p0 + jnp.where(low_lanes, 0.0, r1)).astype(LOW)
+        attn_low[:, base + 128 : base + 256] = jnp.where(low_lanes, r1, r2).astype(LOW)
+        attn_low[:, base + 256 : base + 384] = (p3 + jnp.where(low_lanes, r2, 0.0)).astype(LOW)
+
+    @pl.loop(0, width // 256)
+    def _(m):
+        here = pl.ds(at128(m * 256), 256)
+        go16[here] = dot(attn_low[:, here], cot[pl.ds(0, block)], ROWS_CONTRACT).astype(LOW)
+
+    K_GO = channels(shards)
+    K_GOX = channels(shards)
+    for d in range(shards):
+        send(K_GO + d, go16.at[rows_of(d, other)], go_rx.at[d], ctx=mate(1))
+    attn_branch = dot(attn_low[...], wout[...])
+
+    K_GQA = channels(ctxs)
+    own_gq = gq_tx[my_rows].astype(FULL)
+    for d in planes:
+        arrived(K_GQ + d, gq_rx.at[d])
+        own_gq = own_gq + gq_rx[d].astype(FULL)
+    qkvfin_ref[i] = own_gq.astype(LOW)
+    for e in (1, *even):
+        send(K_GQA + e, qkvfin_ref.at[i], qkvfin_ref.at[i], ctx=mate(e))
+    for d in range(shards):
+        arrived(K_GO + d, go_rx.at[d])
+        total = (go16[rows_of(d, c)].astype(FULL) + go_rx[d].astype(FULL)).astype(LOW)
+        go_tx[d] = total
+        if d:
+            send(K_GOX + d, go_tx.at[d], go_x.at[d], shard=plane(d))
+    for d in planes:
+        arrived(K_GUX + d, line_own.at[up_rows(plane(d))])
+    for q in range(4, 8):
+        near(q)
+        far(q - 4)
+
+    total = x_ref[...].astype(FULL) + attn_branch + out_acc[pl.ds(0, block)]
+    for d in planes:
+        arrived(K_OUT + d, out_rx.at[d])
+        total = total + out_rx[d].astype(FULL)
+    y_ref[...] = total.astype(LOW)
+
+    own_go = go_tx[0].astype(FULL)
+    for d in planes:
+        arrived(K_GOX + d, go_x.at[d])
+        own_go = own_go + go_x[d].astype(FULL)
+    line_own[pl.ds(line_rows - half_rows, half_rows)] = own_go.astype(LOW)
+    near(8)
+    for q in range(4, 8):
+        far(q)
+
+    a2 = a2_acc[pl.ds(0, block)]
+    for d in planes:
+        arrived(K_A2 + d, a2_rx.at[d])
+        a2 = a2 + a2_rx[d].astype(FULL)
+    a1 = a1_c[0].astype(FULL)
+    for k in range(1, ctxs // 2):
+        arrived(K_A1 + k, a1_rx.at[k])
+        a1 = a1 + a1_rx[k].astype(FULL)
+    small_a[0:1] = jnp.sum(a1 * normal, axis=0, keepdims=True)
+    small_a[1:2] = jnp.sum(a1, axis=0, keepdims=True)
+    small_a[2:3] = jnp.sum(a2 * normal, axis=0, keepdims=True)
+    small_a[3:4] = jnp.sum(a2, axis=0, keepdims=True)
+    small_a[5:6, 0:384] = bias_sum
+    small_a[5:6, 384:768] = jnp.zeros((1, 384), FULL)
+    small_a[6:8] = jnp.zeros((2, width), FULL)
+    K_SM = channels(ctxs)
+    K_SMX = channels(shards)
+    for e in mates:
+        send(K_SM + e, small_a, small_rx.at[e], ctx=mate(e))
+    mixed = a1 * gain1_ref[...] + a2 * gain2_ref[...]
+    back = r * (
+        mixed
+        - jnp.mean(mixed, axis=-1, keepdims=True)
+        - normal * jnp.mean(mixed * normal, axis=-1, keepdims=True)
+    )
+    dx_ref[...] = (cot[pl.ds(0, block)].astype(FULL) + back).astype(LOW)
+
+    for e in even:
+        arrived(K_GQA + e, qkvfin_ref.at[mate(e)])
+        send(K_GQA + e + 1, qkvfin_ref.at[mate(e)], qkvfin_ref.at[mate(e)], ctx=mate(1))
+
+    small_rx[0] = small_a[...]
+    for e in mates:
+        arrived(K_SM + e, small_rx.at[e])
+    summed = small_rx[0]
+    for e in mates:
+        summed = summed + small_rx[e]
+    small_b[0, 0:8] = summed
+    for j in range(ctxs):
+        small_b[0, 8 + j : 9 + j] = small_rx[flip(i, j), 5:6]
+    for d in planes:
+        send(K_SMX + d, small_b.at[0], small_b.at[d], shard=plane(d))
+    far(8)
+    for d in planes:
+        arrived(K_SMX + d, small_b.at[d])
+    whole = small_b[0]
+    for d in planes:
+        whole = whole + small_b[d]
+    small_ref[0:16] = whole
+    for j in range(shards):
+        small_ref[16 + j : 17 + j] = small_b[flip(s, j), 4:5]
+    small_ref[20:24] = jnp.zeros((4, width), FULL)
+
+    arrived(K_GQA + 1, qkvfin_ref.at[mate(1)])
+    for e in even:
+        arrived(K_GQA + e + 1, qkvfin_ref.at[mate(e + 1)])
+    for q in range(chunks):
+        arrived(K_FIN + q, fin_ref.at[other, span_of(q)])
+    for copy in sent:
+        copy.wait_send()
+    for q in range(chunks):
+        near_copy(q, line_own).wait_send()
+
+        @pl.when(jnp.logical_not(is_end))
+        def _():
+            far_copy(q).wait_send()
+
+
+def ring_on_device(
     layer_input,
     positions,
     cotangent,
@@ -304,6 +949,184 @@
     )
 
 
+def fused_on_device(
+    layer_input,
+    positions,
+    cotangent,
+    ln1_gain,
+    ln1_bias,
+    ln2_gain,
+    ln2_bias,
+    w_qkv,
+    qkv_bias,
+    w_out,
+    w_up,
+    up_bias,
+    w_down,
+):
+    shards, ctxs = lax.axis_size("shard"), lax.axis_size("ctx")
+    block, width = layer_input.shape[1:]
+    rows = w_qkv.shape[0]
+    i = lax.axis_index("ctx")
+    first = HEAD_DIM * (3 * (i // 2) + i % 2)
+    wsel = lax.dynamic_slice(
+        w_qkv.reshape(rows, 3, width), (0, 0, first), (rows, 3, 2 * HEAD_DIM)
+    ).reshape(rows, 6 * HEAD_DIM)
+    bsel = lax.dynamic_slice(
+        qkv_bias.reshape(3, width), (0, first), (3, 2 * HEAD_DIM)
+    ).reshape(1, 6 * HEAD_DIM)
+    line_rows = width // 2 + rows * shards // 2 + rows // 2
+    vmem = pl.BlockSpec(memory_space=pltpu.VMEM)
+    hbm = pl.BlockSpec(memory_space=pl.ANY)
+    low, full = (lambda *shape: pltpu.VMEM(shape, LOW)), (lambda *shape: pltpu.VMEM(shape, FULL))
+    half = rows // 2
+    scratch = [
+        low(width, 384),
+        low(width, width),
+        low(width, width),
+        low(width, width),
+        low(ctxs * block, width),
+        low(shards * block, width),
+        low(shards * block, width),
+        pltpu.VMEM((8, block), jnp.int32),
+        pltpu.VMEM((ctxs, 8, block), jnp.int32),
+        pltpu.SMEM((ctxs, 8, block), jnp.int32),
+        full(ctxs, block, 384),
+        low(ctxs * block, 128),
+        low(ctxs * block, 128),
+        low(ctxs * block, 128),
+        low(ctxs, block, 128),
+        low(ctxs, block, 128),
+        low(ctxs * block, 128),
+        full(ctxs, block, 128),
+        full(ctxs * block, 128),
+        full(ctxs * block, 128),
+        full(ctxs * block, 128),
+        low(ctxs, block, 384),
+        low(ctxs * block, 384),
+        low(ctxs, block, 128),
+        low(ctxs, block, 128),
+        low(block, width),
+        low(ctxs * block, width),
+        low(ctxs // 2, block, width),
+        low(ctxs // 2, block, width),
+        low(ctxs // 2, block, width),
+        low(width, 384),
+        low(shards, rows, 384),
+        low(rows, 384),
+        full(shards * block, width),
+        full(shards * block, width),
+        low(shards, block, width),
+        low(shards, block, width),
+        low(shards, block, width),
+        low(shards, block, width),
+        low(width, width),
+        low(width // 2, width),
+        low(width, width),
+        low(shards, half, width),
+        low(shards, half, width),
+        low(width, width),
+        low(shards, half, width),
+        low(shards, half, width),
+        low(shards, half, width),
+        low(line_rows, width),
+        low(2, line_rows, width),
+        low(line_rows, width),
+        low(line_rows, width),
+        full(8, width),
+        full(ctxs, 8, width),
+        full(shards, 16, width),
+        full(shards, 16, width),
+        pltpu.SemaphoreType.DMA((256,)),
+        pltpu.SemaphoreType.DMA((256,)),
+        pltpu.SemaphoreType.DMA((8,)),
+    ]
+    row = lambda vector: vector.reshape(1, -1)
+    y, dx, fin, qkvfin, small = pl.pallas_call(
+        fused_body,
+        out_shape=(
+            jax.ShapeDtypeStruct((block, width), LOW),
+            jax.ShapeDtypeStruct((block, width), LOW),
+            jax.ShapeDtypeStruct((2, line_rows, width), LOW),
+            jax.ShapeDtypeStruct((ctxs, rows, 384), LOW),
+            jax.ShapeDtypeStruct((24, width), FULL),
+        ),
+        in_specs=[vmem] * 9 + [hbm] * 5,
+        out_specs=(vmem,) * 5,
+        scratch_shapes=scratch,
+        compiler_params=pltpu.CompilerParams(
+            collective_id=0, has_side_effects=True, vmem_limit_bytes=60 * 1024 * 1024
+        ),
+        name="layer",
+    )(
+        layer_input[0],
+        positions,
+        row(ln1_gain),
+        row(ln1_bias),
+        row(ln2_gain),
+        row(ln2_bias),
+        bsel,
+        row(up_bias),
+        jnp.asarray(rotary_constants(ctxs, block)),
+        cotangent[0],
+        wsel,
+        w_up,
+        w_out,
+        w_down,
+    )
+    fin = fin.astype(FULL)
+    cut = width // 2
+    grad_down = fin[:, :cut].reshape(width, width)
+    grad_up = (
+        fin[:, cut : cut + shards * half]
+        .reshape(2, shards, half, width)
+        .transpose(0, 2, 1, 3)
+        .reshape(rows, shards * width)
+    )
+    grad_out = fin[:, cut + shards * half :].reshape(rows, width)
+
+    def heads_of(slabs, count):
+        slabs = slabs.astype(FULL).reshape(ctxs // 2, 2, count, 3, 2, HEAD_DIM)
+        one = slabs[:, 0, :, :, 0]
+        two = slabs[:, 0, :, :, 1] + slabs[:, 1, :, :, 0]
+        three = slabs[:, 1, :, :, 1]
+        return (
+            jnp.stack([one, two, three], axis=3).transpose(1, 2, 0, 3, 4).reshape(count, 3 * width)
+        )
+
+    return (
+        y[None],
+        dx[None],
+        small[0],
+        small[1],
+        small[2],
+        small[3],
+        heads_of(qkvfin, rows),
+        heads_of(small[8 : 8 + ctxs, :384], 1).reshape(-1),
+        grad_out,
+        grad_up,
+        small[16 : 16 + shards].reshape(-1),
+        grad_down,
+    )
+
+
+def on_device(layer_input, positions, cotangent, *params):
+    shards, ctxs = lax.axis_size("shard"), lax.axis_size("ctx")
+    seqs, block, width = layer_input.shape
+    rows, ff = params[4].shape[0], params[7].shape[1]
+    fits = (
+        seqs == 1
+        and block == 128
+        and (shards, ctxs) == (4, 8)
+        and 3 * ctxs == 2 * HEADS
+        and HEAD_DIM == 64
+        and rows * shards == width == HEADS * HEAD_DIM
+        and ff == shards * width
+    )
+    path = fused_on_device if fits else ring_on_device
+    return path(layer_input, positions, cotangent, *params)
+
+
 def solution(mesh):
     placed = (
         P("shard", "ctx", None),

time: 604 us -> 181 us (0.30)
  waiting for transfers between devices: 408 us -> 0 us
  Pallas kernels: 0 us -> 152 us
  blocking collectives: 59 us -> 0 us
  matrix products: 49.6 us -> 0 us
  other arithmetic: 40.6 us -> 0.39 us
  local copies, waits for them, and re-layouts: 4.76 us -> 27.5 us
  loops' own time: 19.8 us -> 0 us
  between operations: 15.6 us -> 0.77 us
    ppermute x44 -> x0, waiting for transfers between devices: 157 us -> none  [shifted(): lax.ppermute(shard, axis, [(i, (i + by) % count) for i in range(count)])]
    reduce_scatter x4 -> x0, waiting for transfers between devices: 156 us -> none  [the longest x1 60 us: on_device(): lax.psum_scatter(summed[2].astype(jnp.bfloat16), 'shard', scatter_dimensi...]
    pallas_call x0 -> x1, Pallas kernels: none -> 152 us  [fused_on_device(): pl.pallas_call(fused_body, out_shape=(jax.ShapeDtypeStruct((block, width)...]
    all_gather x4 -> x0, waiting for transfers between devices: 60.2 us -> none  [the longest x1 47 us: on_device(): lax.all_gather(w_qkv, 'shard', axis=0, tiled=True)]
    dot_general x40 -> x0, matrix products: 49.6 us -> none  [the longest x1 8.35 us: on_device(): jnp.dot(normed_two, whole_up, preferred_element_type=jnp.float32) + up_bias]
    psum x2 -> x0, blocking collectives: 45 us -> none  [the longest x1 29.7 us: on_device(): lax.psum(grad_gain_one.astype(jnp.bfloat16), 'ctx').astype(jnp.float32)]
    psum x1 -> x0, waiting for transfers between devices: 32.2 us -> none  [on_device(): lax.psum(grad_qkv.astype(jnp.bfloat16), 'ctx').astype(jnp.float32)]
    another operation x18 -> x0, loops' own time: 19.8 us -> none  [the longest x1 9.94 us: on_device(): lax.fori_loop(1, cycle_size, cycle_backward, (grad_query, key_rows, value...]
  transfers between devices with their start and end apart: 53 -> 0, of which waited for: 50 -> 0; matrix products, arithmetic and copies ran while one was open for 14% -> 0% of each run, Pallas kernels for 0% -> 0%
where the time goes in v1:
time: 181 us
  Pallas kernels  152 us (84%)
  local copies, waits for them, and re-layouts  27.5 us (15%)
    pallas_call x1, Pallas kernels, fused_on_device(): pl.pallas_call(fused_body, out_shape=(jax.ShapeDtypeStruct((block, width)...  152 us
    unnamed x15, local copies, waits for them, and re-layouts  7.57 us
    reshape x4, local copies, waits for them, and re-layouts, fused_on_device(): row = lambda vector: vector.reshape(1, -1)  5.07 us

profile of v1, /device:TPU:0, one launch (start us, length us, event | category | flops | bytes accessed | tf_op | source)
XLA Modules:
  0.0 180.7 jit_solution(12208767852104064996)
XLA Ops:
  0.6 1.3 reshape.119.gain1_ref
  1.9 1.3 reshape.120.bias1_ref
  3.2 1.3 reshape.121.gain2_ref
  4.4 1.3 reshape.122.bias2_ref
  5.7 0.7 reshape.123
  6.5 0.6 copy.57
  7.1 2.2 %reshape.126 = bf16[192,3,768]{2,1,0:T(4,128)(2,1)S(1)} reshape(bf16[192,2304]{1,0:T(8,128)(2,1)} %param.21) | data formatting | bytes 1769472 | tf_op jit(solution)/shard_map/reshape | solution.py:973
  9.5 0.7 copy.56
  10.1 152.0 %layer.1 = (bf16[128,768]{1,0:T(8,128)(2,1)}, bf16[128,768]{1,0:T(8,128)(2,1)}, bf16[2,864,768]{2,1,0:T(8,128)(2,1)}, bf16[8,192,384]{2,1,0:T(8,128)(2,1)}, f32[24,768]{1,0:T(8,128)}) custom-call(bf16[128,768]{1,0:T(8,128)(2,1)} %bitcast.60, s32[1,128]{1,0:T(1,128)} %pos_ref.1, f32[1,768]{1,0:T(1,128)} %reshape.119.gain1_ref, f32[1,768]{1,0:T(1,128)} %reshape.120.bias1_ref, ...), custom_call_target="tpu_custom_call" | custom-call | tf_op jit(solution)/shard_map/layer/pallas_call | solution.py:1045
  162.1 1.6 slice_reduce_fusion
  163.7 1.6 copy.31
  165.6 0.3 maximum_bitcast_fusion
  165.8 1.6 copy.35
  167.4 3.1 %copy.41 = f32[192,2304]{1,0:T(8,128)} copy(f32[192,2304]{0,1:T(8,128)} %bitcast.52) | data formatting | bytes 3538944
  170.5 0.7 slice.59
  171.4 0.7 reshape_reshape.3
  172.0 0.9 slice.76
  172.9 1.7 fusion.2
  174.6 1.5 copy.40
  176.1 1.8 %copy.51 = f32[24,8,4,768]{3,1,2,0:T(8,128)} copy(f32[24,8,4,768]{3,2,1,0:T(4,128)S(1)} %bitcast.53) | data formatting | bytes 4718592
  178.0 0.7 slice.66
  178.7 0.6 reshape.135
  179.3 0.7 copy.60
  180.0 0.7 copy.61
  (16 shorter events, 0.6 us)
Async XLA Ops:
  167.4 4.6 %copy-start = (bf16[2,864,768]{2,1,0:T(8,128)(2,1)S(1)}, bf16[2,864,768]{2,1,0:T(8,128)(2,1)}, u32[]{:S(2)}) copy-start(bf16[2,864,768]{2,1,0:T(8,128)(2,1)} %get-tuple-element.21) | copy-start | bytes 7962628
  176.1 3.2 %copy-start.2 = (bf16[128,768]{1,0:T(8,128)(2,1)S(1)}, bf16[128,768]{1,0:T(8,128)(2,1)}, u32[]{:S(2)}) copy-start(bf16[128,768]{1,0:T(8,128)(2,1)} %get-tuple-element.17) | copy-start | bytes 589828
  176.1 3.9 %copy-start.1 = (bf16[128,768]{1,0:T(8,128)(2,1)S(1)}, bf16[128,768]{1,0:T(8,128)(2,1)}, u32[]{:S(2)}) copy-start(bf16[128,768]{1,0:T(8,128)(2,1)} %get-tuple-element.18) | copy-start | bytes 589828

commit v2 on v0

--- a/solution.py
+++ b/solution.py
@@ -1,6 +1,11 @@
+import functools
+
 import jax
 import jax.numpy as jnp
+import numpy as np
 from jax import lax
+from jax.experimental import pallas as pl
+from jax.experimental.pallas import tpu as pltpu
 from jax.sharding import PartitionSpec as P
 
 HEADS = 12
@@ -51,7 +56,793 @@
     return jax.nn.gelu(field_in, approximate=False)
 
 
-def on_device(
+MESH = pl.DeviceIdType.MESH
+LOW = jnp.bfloat16
+FULL = jnp.float32
+ROWS_CONTRACT = (((0,), (0,)), ((), ()))
+COLS_CONTRACT = (((1,), (1,)), ((), ()))
+INV_ROOT_TWO = 0.7071067811865476
+INV_ROOT_TWO_PI = 0.3989422804014327
+CHUNK = 48
+LAG = 2
+
+
+def dot(lhs, rhs, dims=(((1,), (0,)), ((), ()))):
+    return lax.dot_general(lhs, rhs, dims, preferred_element_type=FULL)
+
+
+def flip(index, bits):
+    for power in (1, 2, 4, 8):
+        if bits & power:
+            index = index + power - 2 * power * lax.rem(lax.div(index, power), 2)
+    return index
+
+
+def at16(value):
+    return pl.multiple_of(value, 16)
+
+
+def at128(value):
+    return pl.multiple_of(value, 128)
+
+
+def rotary_constants(blocks, block_len):
+    lane = np.arange(128) % HEAD_DIM
+    half = ROTARY // 2
+    turning = lane < ROTARY
+    freq = np.where(turning, 10000.0 ** (-(lane % half) * (2.0 / ROTARY)), 0.0)
+    sign = np.where(lane < half, -1.0, 1.0) * turning
+    offset = np.arange(block_len)[:, None] * freq
+    start = (np.arange(blocks) * block_len)[:, None] * freq
+    parts = (np.cos(offset), np.sin(offset) * sign, np.cos(start), np.sin(start) * sign)
+    return np.concatenate(parts).astype(np.float32)
+
+
+def fused_body(names, *refs):
+    (
+        x_ref, pos_ref, gain1_ref, bias1_ref, gain2_ref, bias2_ref, qkvb_ref, upb_ref, rot_ref,
+        cot_hbm, wqkv_hbm, wup_hbm, wout_hbm, wdn_hbm,
+        y_ref, dx_ref, fin_ref, qkvfin_ref, early_ref, late_ref,
+    ) = refs[:20]
+    scratch = dict(zip(names, refs[20:]))
+    run_layer(
+        x_ref, pos_ref, gain1_ref, bias1_ref, gain2_ref, bias2_ref, qkvb_ref, upb_ref, rot_ref,
+        cot_hbm, wqkv_hbm, wup_hbm, wout_hbm, wdn_hbm,
+        y_ref, dx_ref, fin_ref, qkvfin_ref, early_ref, late_ref, **scratch,
+    )
+
+
+def run_layer(
+    x_ref, pos_ref, gain1_ref, bias1_ref, gain2_ref, bias2_ref, qkvb_ref, upb_ref, rot_ref,
+    cot_hbm, wqkv_hbm, wup_hbm, wout_hbm, wdn_hbm,
+    y_ref, dx_ref, fin_ref, qkvfin_ref, early_ref, late_ref,
+    *,
+    wq, wraw, wup, wout, wdn, n1, n2, cot, pos_tx, pos_rx, pos_sm, qkv, q_s, k_s, v_s, do_tx, do_mid, do_rx, do_s,
+    o_s, dq_s, dk_s, dv_s, gp_s, gp_e, o_tx, o_rx, attn, a1_p, a1_d2d, a1_own, a1_tx_r, a1_tx_l, a1_rx_r, a1_rx_l,
+    gq_tx, gq_rx, out_acc, a2_acc, out_tx, out_rx, a2_tx, a2_rx, gd16, gd_rx, gu16, gu_rx, gu_tx,
+    go16, go_rx, line_own, line_rx, line_near, line_far, early_a, early_rx, early_b,
+    late_a, late_rx, late_b, ssem, rsem, lsem,
+):
+    shards = lax.axis_size("shard")
+    ctxs = lax.axis_size("ctx")
+    s = lax.axis_index("shard")
+    i = lax.axis_index("ctx")
+    c = lax.rem(i, 2)
+    z = lax.div(i, 2)
+    other = 1 - c
+    Z = ctxs // 2
+    planes = range(1, shards)
+    mates = range(1, ctxs)
+    block = x_ref.shape[0]
+    width = x_ref.shape[1]
+    rows = width // shards
+    half_rows = rows // 2
+    half_width = width // 2
+    sent = []
+    used = [0]
+    always = None
+
+    def channels(count):
+        first = used[0]
+        used[0] += count
+        return first
+
+    def copy_of(send_k, recv_k, src, dst, device):
+        return pltpu.make_async_remote_copy(
+            src_ref=src,
+            dst_ref=dst,
+            send_sem=ssem.at[send_k],
+            recv_sem=rsem.at[recv_k],
+            device_id=device,
+            device_id_type=MESH,
+        )
+
+    def send(k, src, dst, device, recv_k=None, when=always):
+        copy = copy_of(k, k if recv_k is None else recv_k, src, dst, device)
+        sent.append((copy, when))
+        if when is always:
+            copy.start()
+        else:
+            pl.when(when)(copy.start)
+
+    def arrived(k, dst):
+        copy_of(k, k, dst, dst, {"ctx": flip(i, 1)}).wait_recv()
+
+    def plane(d):
+        return flip(s, d)
+
+    def mate(e):
+        return flip(i, e)
+
+    partner = {"ctx": flip(i, 1)}
+    right = {"ctx": i + 2}
+    left = {"ctx": i - 2}
+    has_left = z > 0
+    has_right = z < Z - 1
+
+    loads = []
+
+    def load(src, dst):
+        copy = pltpu.make_async_copy(src, dst, lsem.at[len(loads)])
+        copy.start()
+        loads.append(copy)
+
+    my_rows = pl.ds(at16(s * rows), rows)
+    first = HEAD_DIM * (3 * z + c)
+    base = jnp.minimum(128 * lax.div(first, 128), width - 256)
+    for part in range(3):
+        load(wqkv_hbm.at[:, pl.ds(at128(width * part + base), 256)], wraw.at[part])
+    load(cot_hbm, cot.at[pl.ds(0, block)])
+    load(wout_hbm.at[pl.ds(0, 128)], wout.at[pl.ds(0, 128)])
+    load(wout_hbm.at[pl.ds(HEAD_DIM, 128)], wout.at[pl.ds(128, 128)])
+    load(wup_hbm.at[:, pl.ds(at128(s * width), width)], wup.at[my_rows])
+    load(wdn_hbm, wdn)
+
+    barrier = pltpu.get_barrier_semaphore()
+    for d in range(shards):
+        for e in range(ctxs):
+            if d or e:
+                pl.semaphore_signal(
+                    barrier,
+                    inc=1,
+                    device_id={"shard": plane(d), "ctx": mate(e)},
+                    device_id_type=MESH,
+                )
+    pl.semaphore_wait(barrier, shards * ctxs - 1)
+
+    K_COT = channels(shards)
+    K_WQ = channels(shards)
+    K_WU = channels(shards)
+    K_WU2 = channels(shards)
+    K_N2 = channels(shards)
+    K_POS = channels(ctxs)
+    for d in planes:
+        send(K_COT + d, cot_hbm, cot.at[pl.ds(block * d, block)], {"shard": plane(d)})
+
+    def two_heads(here, there):
+        wide = lax.broadcasted_iota(jnp.int32, here.shape, 1)
+        turned = jnp.where(
+            wide < HEAD_DIM, pltpu.roll(here, HEAD_DIM, 1), pltpu.roll(there, HEAD_DIM, 1)
+        )
+        return jnp.where(
+            first == base, here, jnp.where(first == base + HEAD_DIM, turned, there)
+        )
+
+    for copy in loads[:3]:
+        copy.wait()
+    for part in range(3):
+        raw = wraw[part].astype(FULL)
+        wq[my_rows, 128 * part : 128 * (part + 1)] = two_heads(raw[:, :128], raw[:, 128:]).astype(LOW)
+    qkv_bias = jnp.concatenate(
+        [
+            two_heads(
+                jnp.broadcast_to(qkvb_ref[pl.ds(at128(width * part + base), 128)][None, :], (8, 128)),
+                jnp.broadcast_to(qkvb_ref[pl.ds(at128(width * part + base + 128), 128)][None, :], (8, 128)),
+            )
+            for part in range(3)
+        ],
+        axis=1,
+    )[:1]
+    gain1, gain2 = gain1_ref[...][None, :], gain2_ref[...][None, :]
+    bias1, bias2 = bias1_ref[...][None, :], bias2_ref[...][None, :]
+    pos_tx[...] = jnp.broadcast_to(pos_ref[...], pos_tx.shape)
+    x = x_ref[...].astype(FULL)
+    mean = jnp.mean(x, axis=-1, keepdims=True)
+    centered = x - mean
+    r = lax.rsqrt(jnp.mean(centered * centered, axis=-1, keepdims=True) + EPSILON)
+    normal = centered * r
+
+    def tokens(j):
+        return pl.ds(at128(block * j), block)
+
+    n1[tokens(i)] = (normal * gain1 + bias1).astype(LOW)
+    n2[pl.ds(0, block)] = (normal * gain2 + bias2).astype(LOW)
+    pos_rx[i] = pos_tx[...]
+    for e in mates:
+        send(K_POS + e, pos_tx, pos_rx.at[i], {"ctx": mate(e)})
+
+    class Relay:
+        def __init__(self, piece):
+            self.piece = piece
+            self.direct = channels(Z)
+            self.across = channels(2 * Z)
+            self.to_right = channels(Z)
+            self.to_left = channels(Z)
+
+        def begin(self):
+            mine = self.piece(i)
+            send(self.to_right, mine, mine, right, self.direct + z, has_right)
+            send(self.to_left, mine, mine, left, self.direct + z, has_left)
+            send(self.across, mine, mine, partner, self.across + z)
+
+        def step(self, k):
+            @pl.when(z >= k)
+            def _():
+                arrived(self.direct + z - k, self.piece(i - 2 * k))
+
+            piece = self.piece(i - 2 * k)
+            if k < Z - 1:
+                send(self.to_right + k, piece, piece, right, self.direct + z - k, (z >= k) & has_right)
+            send(self.across + 2 * k - 1, piece, piece, partner, self.across + z - k, z >= k)
+
+            @pl.when(z + k < Z)
+            def _():
+                arrived(self.direct + z + k, self.piece(i + 2 * k))
+
+            piece = self.piece(i + 2 * k)
+            if k < Z - 1:
+                send(self.to_left + k, piece, piece, left, self.direct + z + k, (z + k < Z) & has_left)
+            send(self.across + 2 * k, piece, piece, partner, self.across + z + k, z + k < Z)
+
+        def end(self):
+            for to in range(Z):
+                arrived(self.across + to, self.piece(2 * to + other))
+
+    normed = Relay(lambda j: n1.at[tokens(j)])
+    normed.begin()
+    for copy in loads[3:]:
+        copy.wait()
+
+    K_DO = channels(ctxs)
+    K_DOS = channels(ctxs)
+    K_DOM = channels(shards)
+
+    def grad_attn(d):
+        if d:
+            arrived(K_COT + d, cot.at[pl.ds(block * d, block)])
+        field = dot(cot[pl.ds(block * d, block)], wout[...], COLS_CONTRACT)
+        for core in range(2):
+            do_tx[d, core] = field[:, 128 * core : 128 * (core + 1)].astype(LOW)
+        if d:
+            send(K_DOM + d, do_tx.at[d], do_mid.at[d], {"shard": plane(d)})
+        else:
+            do_mid[0] = do_tx[0]
+
+    def grad_attn_on(d):
+        if d:
+            arrived(K_DOM + d, do_mid.at[d])
+        for core in range(2):
+            target = 2 * plane(d) + core
+            piece = do_mid.at[d, core]
+            send(K_DOS + 2 * d + core, piece, do_rx.at[i], {"ctx": target}, K_DO + i, i != target)
+
+            @pl.when(i == target)
+            def _():
+                do_rx[i] = do_mid[d, core]
+
+    def send_wq(d):
+        send(K_WQ + d, wq.at[my_rows], wq.at[my_rows], {"shard": plane(d)})
+
+    near_planes, last_plane = planes[:-1], planes[-1]
+    for d in (0, *near_planes):
+        grad_attn(d)
+    for d in near_planes:
+        send_wq(d)
+    normed.step(1)
+    grad_attn_on(0)
+    grad_attn(last_plane)
+    send_wq(last_plane)
+    my_half = pl.ds(at16(s * rows + c * half_rows), half_rows)
+    for d in planes:
+        send(
+            K_WU + d,
+            wup_hbm.at[
+                pl.ds(at16(c * half_rows), half_rows), pl.ds(at128(plane(d) * width), width)
+            ],
+            wup.at[my_half],
+            {"shard": plane(d)},
+        )
+    for d in planes:
+        send(K_N2 + d, n2.at[pl.ds(0, block)], n2.at[pl.ds(block * d, block)], {"shard": plane(d)})
+    for d in near_planes:
+        grad_attn_on(d)
+    normed.step(2)
+    grad_attn_on(last_plane)
+    for k in range(3, Z):
+        normed.step(k)
+    normed.end()
+    for d in planes:
+        arrived(K_WQ + d, wq.at[pl.ds(at16(plane(d) * rows), rows)])
+
+    @pl.loop(0, ctxs // 2)
+    def _(m):
+        here = pl.ds(at128(m * 2 * block), 2 * block)
+        qkv[pl.ds(2 * m, 2)] = dot(n1[here], wq[...]).reshape(2, block, 384)
+
+    for e in mates:
+        arrived(K_POS + e, pos_rx.at[mate(e)])
+    to_scalar = pltpu.make_async_copy(pos_rx, pos_sm, lsem.at[len(loads)])
+    to_scalar.start()
+    to_scalar.wait()
+    rank = [lax.div(pos_sm[j, 0, 0], block) for j in range(ctxs)]
+    place = []
+    for g in range(ctxs):
+        found = jnp.int32(0)
+        for j in range(1, ctxs):
+            found = found + j * (rank[j] == g).astype(jnp.int32)
+        place.append(lax.rem(found, ctxs))
+
+    lane = lax.broadcasted_iota(jnp.int32, (block, 128), 1)
+    leads = lax.rem(lane, HEAD_DIM) < ROTARY // 2
+
+    def across(field):
+        return jnp.where(
+            leads,
+            pltpu.roll(field, 128 - ROTARY // 2, 1),
+            pltpu.roll(field, ROTARY // 2, 1),
+        )
+
+    def tables(g):
+        off_cos, off_sin = rot_ref[pl.ds(0, block)], rot_ref[pl.ds(block, block)]
+        start_cos = rot_ref[pl.ds(2 * block + g, 1)]
+        start_sin = rot_ref[pl.ds(2 * block + ctxs + g, 1)]
+        cosine = start_cos * off_cos - start_sin * off_sin
+        sine = start_sin * off_cos + start_cos * off_sin
+        return cosine, sine
+
+    for j in range(ctxs):
+
+        @pl.when(j != i)
+        def _():
+            arrived(K_DO + j, do_rx.at[j])
+
+    for g in range(ctxs):
+        here = pl.ds(block * g, block)
+        field = qkv[place[g]] + qkv_bias
+        cosine, sine = tables(g)
+        q_raw, k_raw = field[:, :128], field[:, 128:256]
+        turned_q = (q_raw * cosine + across(q_raw) * sine).astype(LOW)
+        q_s[here] = turned_q * jnp.asarray(HEAD_DIM**-0.5, LOW)
+        k_s[here] = (k_raw * cosine + across(k_raw) * sine).astype(LOW)
+        v_s[here] = field[:, 256:].astype(LOW)
+        do_s[here] = do_rx[place[g]]
+
+    o_s[...] = jnp.zeros_like(o_s)
+    dq_s[...] = jnp.zeros_like(dq_s)
+    dk_s[...] = jnp.zeros_like(dk_s)
+    dv_s[...] = jnp.zeros_like(dv_s)
+
+    @pl.loop(0, 2)
+    def _(h):
+        mine = lax.div(lane, HEAD_DIM) == h
+        for g in range(ctxs):
+            share = 0 if g % 4 in (0, 3) else 1
+
+            @pl.when((h == c) | (c == share))
+            def _():
+                here = pl.ds(block * g, block)
+                upto = pl.ds(0, block * (g + 1))
+                span = block * (g + 1)
+                zero = jnp.zeros((block, 128), LOW)
+                q_h = jnp.where(mine, q_s[here], zero)
+                do_h = jnp.where(mine, do_s[here], zero)
+                scores = dot(q_h, k_s[upto], COLS_CONTRACT)
+                token = lax.broadcasted_iota(jnp.int32, (block, span), 0) + block * g
+                key = lax.broadcasted_iota(jnp.int32, (block, span), 1)
+                masked = jnp.where(key <= token, scores, NEGATIVE)
+                top = jnp.max(masked, axis=-1, keepdims=True)
+                weight = jnp.exp(masked - top)
+                probability = weight * (1.0 / jnp.sum(weight, axis=-1, keepdims=True))
+                prob_low = probability.astype(LOW)
+                attended = jnp.where(mine, dot(prob_low, v_s[upto]), 0.0)
+                o_s[g] += attended
+                grad_prob = dot(do_h, v_s[upto], COLS_CONTRACT)
+                row_delta = jnp.sum(do_h.astype(FULL) * attended, axis=-1, keepdims=True)
+                grad_score = (probability * (grad_prob - row_delta)).astype(LOW)
+                dq_s[here] += jnp.where(mine, dot(grad_score, k_s[upto]), 0.0)
+                dk_s[upto] += dot(grad_score, q_h, ROWS_CONTRACT)
+                dv_s[upto] += dot(prob_low, do_h, ROWS_CONTRACT)
+
+    K_O = channels(2 * shards)
+    K_OS = channels(ctxs)
+    for j in range(ctxs):
+        o_tx[j] = o_s[rank[j]].astype(LOW)
+        away = (s != z) | (j != i)
+        send(K_OS + j, o_tx.at[j], o_rx.at[2 * s + c], {"shard": z, "ctx": j}, K_O + 2 * s + c, away)
+
+        @pl.when(jnp.logical_not(away))
+        def _():
+            o_rx[2 * s + c] = o_tx[j]
+
+    bias_sum = jnp.zeros((1, 384), FULL)
+    for g in range(ctxs):
+        here = pl.ds(block * g, block)
+        cosine, sine = tables(g)
+        dq = dq_s[here] * (HEAD_DIM**-0.5)
+        dk = dk_s[here]
+        parts = (dq * cosine - across(dq) * sine, dk * cosine - across(dk) * sine, dv_s[here])
+        part = jnp.concatenate(parts, axis=1).astype(LOW)
+        gp_s[g] = part
+        bias_sum = bias_sum + jnp.sum(part.astype(FULL), axis=0, keepdims=True)
+    for j in range(ctxs):
+        gp_e[pl.ds(block * j, block)] = gp_s[rank[j]]
+
+    @pl.loop(0, ctxs // 2)
+    def _(m):
+        here = pl.ds(at128(m * 2 * block), 2 * block)
+        a1_p[pl.ds(2 * m, 2)] = (
+            dot(gp_e[here], wq[...], COLS_CONTRACT).astype(LOW).reshape(2, block, width)
+        )
+
+    K_A1D = channels(Z)
+    for t in range(Z):
+        send(K_A1D + t, a1_p.at[2 * t + other], a1_d2d.at[t], partner)
+
+    @pl.loop(0, width // 256)
+    def _(m):
+        here = pl.ds(at128(m * 256), 256)
+        gq_tx[here] = dot(n1[:, here], gp_e[...], ROWS_CONTRACT).astype(LOW)
+
+    K_GQ = channels(shards)
+    for d in planes:
+        send(
+            K_GQ + d, gq_tx.at[pl.ds(at16(plane(d) * rows), rows)], gq_rx.at[d], {"shard": plane(d)}
+        )
+
+    for t in range(Z):
+        arrived(K_A1D + t, a1_d2d.at[t])
+        a1_own[t] = (a1_p[2 * t + c].astype(FULL) + a1_d2d[t].astype(FULL)).astype(LOW)
+
+    K_A1R = channels(Z)
+    K_A1L = channels(Z)
+
+    def a1_ends():
+        for t in reversed(range(1, Z)):
+            send(K_A1R + t, a1_own.at[t], a1_rx_r.at[t], right, None, z == 0)
+        for t in range(Z - 1):
+            send(K_A1L + t, a1_own.at[t], a1_rx_l.at[t], left, None, z == Z - 1)
+
+    low_side = z < Z // 2
+
+    def a1_right(t, here):
+        when = (z > 0) & (z < t) & here
+
+        @pl.when(when)
+        def _():
+            arrived(K_A1R + t, a1_rx_r.at[t])
+            a1_tx_r[t] = (a1_own[t].astype(FULL) + a1_rx_r[t].astype(FULL)).astype(LOW)
+
+        send(K_A1R + t, a1_tx_r.at[t], a1_rx_r.at[t], right, None, when)
+
+    def a1_left(t, here):
+        when = (z < Z - 1) & (z > t) & here
+
+        @pl.when(when)
+        def _():
+            arrived(K_A1L + t, a1_rx_l.at[t])
+            a1_tx_l[t] = (a1_own[t].astype(FULL) + a1_rx_l[t].astype(FULL)).astype(LOW)
+
+        send(K_A1L + t, a1_tx_l.at[t], a1_rx_l.at[t], left, None, when)
+
+    a1_ends()
+
+    @pl.when(z == 0)
+    def _():
+        a1_rx_r[0] = jnp.zeros((block, width), LOW)
+
+    @pl.when(z == Z - 1)
+    def _():
+        a1_rx_l[Z - 1] = jnp.zeros((block, width), LOW)
+
+    early_a[...] = jnp.zeros_like(early_a)
+    for d in planes:
+        arrived(K_WU + d, wup.at[pl.ds(at16(plane(d) * rows + c * half_rows), half_rows)])
+        part = wup.at[pl.ds(at16(plane(d) * rows + c * half_rows), half_rows)]
+        send(K_WU2 + d, part, part, partner)
+    for d in planes:
+        arrived(K_N2 + d, n2.at[pl.ds(block * d, block)])
+    for d in planes:
+        arrived(K_WU2 + d, wup.at[pl.ds(at16(plane(d) * rows + other * half_rows), half_rows)])
+    out_acc[...] = jnp.zeros_like(out_acc)
+    a2_acc[...] = jnp.zeros_like(a2_acc)
+
+    @pl.loop(0, width // 256)
+    def _(t):
+        units = pl.ds(at128(t * 256), 256)
+        bias = upb_ref[pl.ds(at128(s * width + t * 256), 256)][None, :]
+        pre = dot(n2[...], wup[:, units]) + bias
+        cdf = 0.5 * (1.0 + lax.erf(pre * INV_ROOT_TWO))
+        hidden = (pre * cdf).astype(LOW)
+        slope = cdf + pre * (jnp.exp(-0.5 * pre * pre) * INV_ROOT_TWO_PI)
+        grad_hidden = dot(cot[...], wdn[units], COLS_CONTRACT)
+        grad_pre = (grad_hidden * slope).astype(LOW)
+        early_a[pl.ds(t, 1)] = jnp.sum(grad_pre.astype(FULL), axis=0, keepdims=True)
+        out_acc[...] += dot(hidden, wdn[units])
+        a2_acc[...] += dot(grad_pre, wup[:, units], COLS_CONTRACT)
+        gd16[units] = dot(hidden, cot[...], ROWS_CONTRACT).astype(LOW)
+        gu16[:, units] = dot(n2[...], grad_pre, ROWS_CONTRACT).astype(LOW)
+
+    K_GD = channels(1)
+    K_GU = channels(shards)
+    K_GUX = channels(shards)
+    K_OUT = channels(shards)
+    K_A2 = channels(shards)
+    K_GO = channels(1)
+
+    def rows_of(d, core):
+        return pl.ds(at16(plane(d) * rows + core * half_rows), half_rows)
+
+    for d in range(shards):
+        send(K_GU + d, gu16.at[rows_of(d, other)], gu_rx.at[d], partner)
+    send(K_GD, gd16.at[pl.ds(at16(other * half_width), half_width)], gd_rx, partner)
+    for d in planes:
+        a2_tx[d] = a2_acc[pl.ds(block * d, block)].astype(LOW)
+
+    for seq in range(shards):
+        for core in range(2):
+            k = 2 * seq + core
+
+            @pl.when((seq != s) | (2 * s + core != i))
+            def _():
+                arrived(K_O + k, o_rx.at[k])
+
+            attn[pl.ds(block * seq, block), 128 * core : 128 * (core + 1)] = o_rx[k]
+    for d in range(shards):
+        mine = attn[tokens(plane(d))]
+        total = out_acc[pl.ds(block * d, block)] + dot(mine, wout[...])
+        if d:
+            out_tx[d] = total.astype(LOW)
+        else:
+            out_acc[pl.ds(0, block)] = total
+    go = dot(attn[tokens(plane(0))], cot[pl.ds(0, block)], ROWS_CONTRACT)
+    for d in planes:
+        go = go + dot(attn[tokens(plane(d))], cot[pl.ds(block * d, block)], ROWS_CONTRACT)
+    go16[pl.ds(0, HEAD_DIM)] = go[:HEAD_DIM].astype(LOW)
+    go16[pl.ds(HEAD_DIM, HEAD_DIM)] = (
+        go[HEAD_DIM : 2 * HEAD_DIM] + go[2 * HEAD_DIM : 3 * HEAD_DIM]
+    ).astype(LOW)
+    go16[pl.ds(2 * HEAD_DIM, HEAD_DIM)] = go[3 * HEAD_DIM :].astype(LOW)
+    send(K_GO, go16.at[pl.ds(at16(other * half_rows), half_rows)], go_rx, partner)
+
+    UP = half_width + half_rows
+
+    def up_rows(index):
+        return pl.ds(at16(UP + index * half_rows), half_rows)
+
+    for d in (*planes, 0):
+        arrived(K_GU + d, gu_rx.at[d])
+        total = (gu16[rows_of(d, c)].astype(FULL) + gu_rx[d].astype(FULL)).astype(LOW)
+        if d:
+            gu_tx[d] = total
+            send(K_GUX + d, gu_tx.at[d], line_own.at[up_rows(s)], {"shard": plane(d)})
+        else:
+            line_own[up_rows(s)] = total
+    for d in planes:
+        send(K_A2 + d, a2_tx.at[d], a2_rx.at[d], {"shard": plane(d)})
+    for d in planes:
+        send(K_OUT + d, out_tx.at[d], out_rx.at[d], {"shard": plane(d)})
+
+    is_end = (z == 0) | (z == Z - 1)
+    is_mid = jnp.logical_not(is_end)
+    is_centre = (z == Z // 2 - 1) | (z == Z // 2)
+    inward = jnp.where(z < Z // 2, 2, -2)
+    inner = {"ctx": i + inward}
+    outer = {"ctx": i - inward}
+    to_inner = jnp.where(is_centre, 1, 0)
+    line_rows = half_width + half_rows + shards * half_rows
+    chunks = line_rows // CHUNK
+    first_up = UP // CHUNK
+    K_OUTER = channels(chunks)
+    K_INNER = channels(chunks)
+    K_NEAR = channels(chunks)
+    K_FAR = channels(chunks)
+    K_FIN = channels(chunks)
+
+    def span_of(q):
+        return pl.ds(q * CHUNK, CHUNK)
+
+    def near_end(q):
+        send(
+            K_NEAR + q,
+            line_own.at[span_of(q)],
+            line_rx.at[to_inner, span_of(q)],
+            inner,
+            K_OUTER + chunks * to_inner + q,
+            is_end,
+        )
+
+    def near_mid(q):
+        @pl.when(is_mid)
+        def _():
+            arrived(K_OUTER + q, line_rx.at[0, span_of(q)])
+            line_near[span_of(q)] = (
+                line_rx[0, span_of(q)].astype(FULL) + line_own[span_of(q)].astype(FULL)
+            ).astype(LOW)
+
+        send(
+            K_INNER + q,
+            line_near.at[span_of(q)],
+            line_rx.at[to_inner, span_of(q)],
+            inner,
+            K_OUTER + chunks * to_inner + q,
+            is_mid,
+        )
+
+    def far(q):
+        arrived(K_INNER + q, line_rx.at[1, span_of(q)])
+        beyond = line_rx[1, span_of(q)].astype(FULL) + line_own[span_of(q)].astype(FULL)
+
+        @pl.when(is_mid)
+        def _():
+            line_far[span_of(q)] = beyond.astype(LOW)
+
+        send(
+            K_FAR + q, line_far.at[span_of(q)], line_rx.at[1, span_of(q)], outer, K_INNER + q, is_mid
+        )
+        fin_ref[c, span_of(q)] = (beyond + line_rx[0, span_of(q)].astype(FULL)).astype(LOW)
+        send(K_FIN + q, fin_ref.at[c, span_of(q)], fin_ref.at[c, span_of(q)], partner)
+
+    @pl.when(is_end)
+    def _():
+        line_rx[0] = jnp.zeros((line_rows, width), LOW)
+
+    arrived(K_GD, gd_rx)
+    line_own[pl.ds(0, half_width)] = (
+        gd16[pl.ds(at16(c * half_width), half_width)].astype(FULL) + gd_rx[...].astype(FULL)
+    ).astype(LOW)
+    for q in range(half_width // CHUNK):
+        near_end(q)
+    arrived(K_GO, go_rx)
+    line_own[pl.ds(half_width, half_rows)] = (
+        go16[pl.ds(at16(c * half_rows), half_rows)].astype(FULL) + go_rx[...].astype(FULL)
+    ).astype(LOW)
+    for q in range(half_width // CHUNK, first_up):
+        near_end(q)
+
+    for t in reversed(range(1, Z)):
+        a1_right(t, low_side)
+        a1_left(Z - 1 - t, jnp.logical_not(low_side))
+
+    own_gq = gq_tx[my_rows].astype(FULL)
+    for d in planes:
+        arrived(K_GQ + d, gq_rx.at[d])
+        own_gq = own_gq + gq_rx[d].astype(FULL)
+    qkvfin_ref[i] = own_gq.astype(LOW)
+    spread = Relay(lambda j: qkvfin_ref.at[j])
+
+    for t in reversed(range(1, Z)):
+        a1_right(t, jnp.logical_not(low_side))
+        a1_left(Z - 1 - t, low_side)
+    K_E = channels(ctxs)
+    K_EX = channels(shards)
+    early_a[3:4] = bias_sum[:, :256]
+    early_a[4:5, 0:128] = bias_sum[:, 256:]
+    for e in mates:
+        send(K_E + e, early_a, early_rx.at[e], {"ctx": mate(e)})
+    early_rx[0] = early_a[...]
+
+    for q in range(4):
+        near_mid(q)
+    spread.begin()
+    for d in planes:
+        arrived(K_GUX + d, line_own.at[up_rows(plane(d))])
+    for q in range(first_up, chunks):
+        near_end(q)
+    near_mid(4)
+    far(0)
+    near_mid(5)
+    far(1)
+    near_mid(6)
+    far(2)
+    near_mid(7)
+    far(3)
+    near_mid(8)
+    far(4)
+    near_mid(9)
+    far(5)
+    a1 = a1_own[z].astype(FULL)
+
+    @pl.when(has_left)
+    def _():
+        arrived(K_A1R + z, a1_rx_r.at[z])
+
+    @pl.when(has_right)
+    def _():
+        arrived(K_A1L + z, a1_rx_l.at[z])
+
+    a1 = a1 + a1_rx_r[z].astype(FULL) + a1_rx_l[z].astype(FULL)
+    a2 = a2_acc[pl.ds(0, block)]
+    for d in planes:
+        arrived(K_A2 + d, a2_rx.at[d])
+        a2 = a2 + a2_rx[d].astype(FULL)
+    sums = (a1 * normal, a1, a2 * normal, a2)
+    for k, field in enumerate(sums):
+        total = jnp.sum(field, axis=0, keepdims=True)
+        late_a[2 * k : 2 * k + 1] = total[:, :half_width]
+        late_a[2 * k + 1 : 2 * k + 2] = total[:, half_width:]
+    K_L = channels(ctxs)
+    K_LX = channels(shards)
+    for e in mates:
+        send(K_L + e, late_a, late_rx.at[e], {"ctx": mate(e)})
+    late_rx[0] = late_a[...]
+    mixed = a1 * gain1 + a2 * gain2
+    back = r * (
+        mixed
+        - jnp.mean(mixed, axis=-1, keepdims=True)
+        - normal * jnp.mean(mixed * normal, axis=-1, keepdims=True)
+    )
+    dx_ref[...] = (cot[pl.ds(0, block)].astype(FULL) + back).astype(LOW)
+    for q in range(10, 12):
+        near_mid(q)
+        far(q - 4)
+    spread.step(1)
+    for q in range(12, 15):
+        near_mid(q)
+        far(q - 4)
+    total = x_ref[...].astype(FULL) + out_acc[pl.ds(0, block)]
+    for d in planes:
+        arrived(K_OUT + d, out_rx.at[d])
+        total = total + out_rx[d].astype(FULL)
+    y_ref[...] = total.astype(LOW)
+    for e in mates:
+        arrived(K_E + e, early_rx.at[e])
+    summed = early_rx[0]
+    for e in mates:
+        summed = summed + early_rx[e]
+    early_b[0, 0:8] = summed
+    for j in range(ctxs):
+        early_b[0, 8 + 2 * j : 10 + 2 * j] = early_rx[flip(i, j), 3:5]
+    for e in mates:
+        arrived(K_L + e, late_rx.at[e])
+    summed = late_rx[0]
+    for e in mates:
+        summed = summed + late_rx[e]
+    late_b[0] = summed
+    for d in planes:
+        send(K_EX + d, early_b.at[0], early_b.at[d], {"shard": plane(d)})
+        send(K_LX + d, late_b.at[0], late_b.at[d], {"shard": plane(d)})
+    spread.step(2)
+    for q in range(15, chunks):
+        near_mid(q)
+        far(q - 4)
+    for q in range(chunks - 4, chunks):
+        far(q)
+    for d in planes:
+        arrived(K_EX + d, early_b.at[d])
+        arrived(K_LX + d, late_b.at[d])
+    whole = early_b[0]
+    late = late_b[0]
+    for d in planes:
+        whole = whole + early_b[d]
+        late = late + late_b[d]
+    late_ref[...] = late
+    early_ref[0:24] = whole
+    for j in range(shards):
+        early_ref[24 + 8 * j : 32 + 8 * j] = early_b[flip(s, j), 0:8]
+    for k in range(3, Z):
+        spread.step(k)
+    spread.end()
+    for q in range(chunks):
+        arrived(K_FIN + q, fin_ref.at[other, span_of(q)])
+    assert used[0] <= ssem.shape[0]
+    for copy, when in sent:
+        if when is always:
+            copy.wait_send()
+        else:
+            pl.when(when)(copy.wait_send)
+
+
+def ring_on_device(
     layer_input,
     positions,
     cotangent,
@@ -304,6 +1095,259 @@
     )
 
 
+def finish_body(
+    y_in, dx_in, fin, qkvfin, early, late,
+    y_out, dx_out, g1_out, b1_out, g2_out, b2_out, gqkv_out, gqkvb_out, gout_out, gup_out, gupb_out, gdown_out,
+    gqkv, gout, gup, gdown, sem,
+):
+    width = y_in.shape[1]
+    chips = qkvfin.shape[0] // 2
+    rows = qkvfin.shape[1]
+    half = rows // 2
+    cut = width // 2
+    shards = width // rows
+    slabs = 8 + 4 * chips
+    copies = []
+
+    def out(src, dst):
+        copy = pltpu.make_async_copy(src, dst, sem.at[len(copies)])
+        copy.start()
+        copies.append(copy)
+
+    out(y_in, y_out.at[0])
+    out(dx_in, dx_out.at[0])
+    for h in range(2):
+        gdown[pl.ds(cut * h, cut)] = fin[h, pl.ds(0, cut)].astype(FULL)
+        out(gdown.at[pl.ds(cut * h, cut)], gdown_out.at[pl.ds(cut * h, cut)])
+    for h in range(2):
+        mine = pl.ds(half * h, half)
+        for n in range(shards):
+            here = fin[h, pl.ds(cut + half + half * n, half)]
+            gup[mine, width * n : width * (n + 1)] = here.astype(FULL)
+        out(gup.at[mine], gup_out.at[mine])
+
+    def tiles(piece, wide, put):
+        lane = lax.broadcasted_iota(jnp.int32, wide, 1)
+        low_lanes = lane < HEAD_DIM
+        for part in range(3):
+            for w in range(chips // 2):
+                p0, p1, p2, p3 = (piece(4 * w + t, part) for t in range(4))
+                r1, r2 = pltpu.roll(p1, HEAD_DIM, 1), pltpu.roll(p2, HEAD_DIM, 1)
+                at = width * part + 384 * w
+                put(at, p0 + jnp.where(low_lanes, 0.0, r1))
+                put(at + 128, jnp.where(low_lanes, r1, r2))
+                put(at + 256, p3 + jnp.where(low_lanes, r2, 0.0))
+
+    def put_rows(at, tile):
+        gqkv[:, at : at + 128] = tile
+
+    tiles(
+        lambda j, part: qkvfin[j, :, 128 * part : 128 * (part + 1)].astype(FULL),
+        (rows, 128),
+        put_rows,
+    )
+    out(gqkv, gqkv_out)
+    for h in range(2):
+        gout[pl.ds(half * h, half)] = fin[h, pl.ds(cut, half)].astype(FULL)
+    out(gout, gout_out)
+
+    def bias_piece(j, part):
+        row = early[8 + 2 * j + part // 2, 128 * (part % 2) : 128 * (part % 2 + 1)]
+        return jnp.broadcast_to(row[None, :], (8, 128))
+
+    def put_bias(at, tile):
+        gqkvb_out[pl.ds(at, 128)] = tile[0]
+
+    tiles(bias_piece, (8, 128), put_bias)
+    for n in range(shards):
+        for t in range(width // 256):
+            gupb_out[pl.ds(width * n + 256 * t, 256)] = early[slabs + 8 * n + t]
+    for k, vector in enumerate((g1_out, b1_out, g2_out, b2_out)):
+        vector[pl.ds(0, cut)] = late[2 * k]
+        vector[pl.ds(cut, cut)] = late[2 * k + 1]
+    for copy in copies:
+        copy.wait()
+
+
+def finish(rows, shards, ctxs, *pieces):
+    block, width = pieces[0].shape
+    vmem = pl.BlockSpec(memory_space=pltpu.VMEM)
+    hbm = pl.BlockSpec(memory_space=pl.ANY)
+    shape = jax.ShapeDtypeStruct
+    vector = shape((width,), FULL)
+    return pl.pallas_call(
+        finish_body,
+        out_shape=(
+            shape((1, block, width), LOW),
+            shape((1, block, width), LOW),
+            vector,
+            vector,
+            vector,
+            vector,
+            shape((rows, 3 * width), FULL),
+            shape((3 * width,), FULL),
+            shape((rows, width), FULL),
+            shape((rows, shards * width), FULL),
+            shape((shards * width,), FULL),
+            shape((width, width), FULL),
+        ),
+        in_specs=[vmem] * 6,
+        out_specs=(hbm, hbm, vmem, vmem, vmem, vmem, hbm, vmem, hbm, hbm, vmem, hbm),
+        scratch_shapes=[
+            pltpu.VMEM((rows, 3 * width), FULL),
+            pltpu.VMEM((rows, width), FULL),
+            pltpu.VMEM((rows, shards * width), FULL),
+            pltpu.VMEM((width, width), FULL),
+            pltpu.SemaphoreType.DMA((8,)),
+        ],
+        compiler_params=pltpu.CompilerParams(vmem_limit_bytes=24 * 2**20),
+        name="finish",
+    )(*pieces)
+
+
+def fused_on_device(
+    layer_input,
+    positions,
+    cotangent,
+    ln1_gain,
+    ln1_bias,
+    ln2_gain,
+    ln2_bias,
+    w_qkv,
+    qkv_bias,
+    w_out,
+    w_up,
+    up_bias,
+    w_down,
+):
+    shards, ctxs = lax.axis_size("shard"), lax.axis_size("ctx")
+    block, width = layer_input.shape[1:]
+    rows = w_qkv.shape[0]
+    half = rows // 2
+    line_rows = width // 2 + half + shards * half
+    vmem = pl.BlockSpec(memory_space=pltpu.VMEM)
+    hbm = pl.BlockSpec(memory_space=pl.ANY)
+    low, full = (lambda *shape: pltpu.VMEM(shape, LOW)), (lambda *shape: pltpu.VMEM(shape, FULL))
+    chips = ctxs // 2
+    scratch = dict(
+        wq=low(width, 384),
+        wraw=low(3, rows, 256),
+        wup=low(width, width),
+        wout=low(256, width),
+        wdn=low(width, width),
+        n1=low(ctxs * block, width),
+        n2=low(shards * block, width),
+        cot=low(shards * block, width),
+        pos_tx=pltpu.VMEM((8, block), jnp.int32),
+        pos_rx=pltpu.VMEM((ctxs, 8, block), jnp.int32),
+        pos_sm=pltpu.SMEM((ctxs, 8, block), jnp.int32),
+        qkv=full(ctxs, block, 384),
+        q_s=low(ctxs * block, 128),
+        k_s=low(ctxs * block, 128),
+        v_s=low(ctxs * block, 128),
+        do_tx=low(shards, 2, block, 128),
+        do_mid=low(shards, 2, block, 128),
+        do_rx=low(ctxs, block, 128),
+        do_s=low(ctxs * block, 128),
+        o_s=full(ctxs, block, 128),
+        dq_s=full(ctxs * block, 128),
+        dk_s=full(ctxs * block, 128),
+        dv_s=full(ctxs * block, 128),
+        gp_s=low(ctxs, block, 384),
+        gp_e=low(ctxs * block, 384),
+        o_tx=low(ctxs, block, 128),
+        o_rx=low(2 * shards, block, 128),
+        attn=low(shards * block, 256),
+        a1_p=low(ctxs, block, width),
+        a1_d2d=low(chips, block, width),
+        a1_own=low(chips, block, width),
+        a1_tx_r=low(chips, block, width),
+        a1_tx_l=low(chips, block, width),
+        a1_rx_r=low(chips, block, width),
+        a1_rx_l=low(chips, block, width),
+        gq_tx=low(width, 384),
+        gq_rx=low(shards, rows, 384),
+        out_acc=full(shards * block, width),
+        a2_acc=full(shards * block, width),
+        out_tx=low(shards, block, width),
+        out_rx=low(shards, block, width),
+        a2_tx=low(shards, block, width),
+        a2_rx=low(shards, block, width),
+        gd16=low(width, width),
+        gd_rx=low(width // 2, width),
+        gu16=low(width, width),
+        gu_rx=low(shards, half, width),
+        gu_tx=low(shards, half, width),
+        go16=low(rows, width),
+        go_rx=low(half, width),
+        line_own=low(line_rows, width),
+        line_rx=low(2, line_rows, width),
+        line_near=low(line_rows, width),
+        line_far=low(line_rows, width),
+        early_a=full(8, 256),
+        early_rx=full(ctxs, 8, 256),
+        early_b=full(shards, 8 + 2 * ctxs, 256),
+        late_a=full(8, width // 2),
+        late_rx=full(ctxs, 8, width // 2),
+        late_b=full(shards, 8, width // 2),
+        ssem=pltpu.SemaphoreType.DMA((320,)),
+        rsem=pltpu.SemaphoreType.DMA((320,)),
+        lsem=pltpu.SemaphoreType.DMA((16,)),
+    )
+    slabs = 8 + 2 * ctxs
+    y, dx, fin, qkvfin, early, late = pl.pallas_call(
+        functools.partial(fused_body, tuple(scratch)),
+        out_shape=(
+            jax.ShapeDtypeStruct((block, width), LOW),
+            jax.ShapeDtypeStruct((block, width), LOW),
+            jax.ShapeDtypeStruct((2, line_rows, width), LOW),
+            jax.ShapeDtypeStruct((ctxs, rows, 384), LOW),
+            jax.ShapeDtypeStruct((slabs + 8 * shards, 256), FULL),
+            jax.ShapeDtypeStruct((8, width // 2), FULL),
+        ),
+        in_specs=[vmem] * 9 + [hbm] * 5,
+        out_specs=(vmem,) * 6,
+        scratch_shapes=list(scratch.values()),
+        compiler_params=pltpu.CompilerParams(
+            collective_id=0, has_side_effects=True, vmem_limit_bytes=60 * 1024 * 1024
+        ),
+        name="layer",
+    )(
+        layer_input[0],
+        positions,
+        ln1_gain,
+        ln1_bias,
+        ln2_gain,
+        ln2_bias,
+        qkv_bias,
+        up_bias,
+        jnp.asarray(rotary_constants(ctxs, block)),
+        cotangent[0],
+        w_qkv,
+        w_up,
+        w_out,
+        w_down,
+    )
+    return finish(rows, shards, ctxs, y, dx, fin, qkvfin, early, late)
+
+
+def on_device(layer_input, positions, cotangent, *params):
+    shards, ctxs = lax.axis_size("shard"), lax.axis_size("ctx")
+    seqs, block, width = layer_input.shape
+    rows, ff = params[4].shape[0], params[7].shape[1]
+    fits = (
+        seqs == 1
+        and block == 128
+        and (shards, ctxs) == (4, 8)
+        and 3 * ctxs == 2 * HEADS
+        and HEAD_DIM == 64
+        and rows * shards == width == HEADS * HEAD_DIM
+        and ff == shards * width
+    )
+    path = fused_on_device if fits else ring_on_device
+    return path(layer_input, positions, cotangent, *params)
+
+
 def solution(mesh):
     placed = (
         P("shard", "ctx", None),

time: 604 us -> 134 us (0.22)
  waiting for transfers between devices: 408 us -> 0 us
  Pallas kernels: 0 us -> 126 us
  blocking collectives: 59 us -> 0 us
  matrix products: 49.6 us -> 0 us
  other arithmetic: 40.6 us -> 0 us
  loops' own time: 19.8 us -> 0 us
  between operations: 15.6 us -> 0.83 us
    ppermute x44 -> x0, waiting for transfers between devices: 157 us -> none  [shifted(): lax.ppermute(shard, axis, [(i, (i + by) % count) for i in range(count)])]
    reduce_scatter x4 -> x0, waiting for transfers between devices: 156 us -> none  [the longest x1 60 us: on_device(): lax.psum_scatter(summed[2].astype(jnp.bfloat16), 'shard', scatter_dimensi...]
    pallas_call x0 -> x2, Pallas kernels: none -> 126 us  [the longest x1 122 us: fused_on_device(): pl.pallas_call(functools.partial(fused_body, tuple(scratch)), out_shape=(...]
    all_gather x4 -> x0, waiting for transfers between devices: 60.2 us -> none  [the longest x1 47 us: on_device(): lax.all_gather(w_qkv, 'shard', axis=0, tiled=True)]
    dot_general x40 -> x0, matrix products: 49.6 us -> none  [the longest x1 8.35 us: on_device(): jnp.dot(normed_two, whole_up, preferred_element_type=jnp.float32) + up_bias]
    psum x2 -> x0, blocking collectives: 45 us -> none  [the longest x1 29.7 us: on_device(): lax.psum(grad_gain_one.astype(jnp.bfloat16), 'ctx').astype(jnp.float32)]
    psum x1 -> x0, waiting for transfers between devices: 32.2 us -> none  [on_device(): lax.psum(grad_qkv.astype(jnp.bfloat16), 'ctx').astype(jnp.float32)]
    another operation x18 -> x0, loops' own time: 19.8 us -> none  [the longest x1 9.94 us: on_device(): lax.fori_loop(1, cycle_size, cycle_backward, (grad_query, key_rows, value...]
  transfers between devices with their start and end apart: 53 -> 0, of which waited for: 50 -> 0; matrix products, arithmetic and copies ran while one was open for 14% -> 0% of each run, Pallas kernels for 0% -> 0%
where the time goes in v2:
time: 134 us; the launch traced here: 133 us
  Pallas kernels  126 us (94%)
  local copies, waits for them, and re-layouts  6.39 us (5%)
    pallas_call x1, Pallas kernels, fused_on_device(): pl.pallas_call(functools.partial(fused_body, tuple(scratch)), out_shape=(...  122 us
    unnamed x12, local copies, waits for them, and re-layouts  6.39 us
    pallas_call x1, Pallas kernels, finish(): pl.pallas_call(finish_body, out_shape=(shape((1, block, width), LOW), sha...  3.94 us

profile of v2, /device:TPU:0, one launch (start us, length us, event | category | flops | bytes accessed | tf_op | source)
XLA Modules:
  0.0 133.4 jit_solution(6526455826592743741)
XLA Ops:
  0.6 122.3 %layer.1 = (bf16[128,768]{1,0:T(8,128)(2,1)}, bf16[128,768]{1,0:T(8,128)(2,1)}, bf16[2,864,768]{2,1,0:T(8,128)(2,1)}, bf16[8,192,384]{2,1,0:T(8,128)(2,1)}, f32[56,256]{1,0:T(8,128)}, /*index=5*/f32[8,384]{1,0:T(8,128)}) custom-call(bf16[128,768]{1,0:T(8,128)(2,1)} %bitcast.2, s32[1,128]{1,0:T(1,128)} %refs_1_.1, f32[768]{0:T(1024)} %refs_2_.1, ...), custom_call_target="tpu_custom_call" | custom-call | tf_op jit(solution)/shard_map/layer/pallas_call | solution.py:1298
  122.9 0.0 copy-start
  123.0 1.7 %copy-done = bf16[2,864,768]{2,1,0:T(8,128)(2,1)S(1)} copy-done((bf16[2,864,768]{2,1,0:T(8,128)(2,1)S(1)}, bf16[2,864,768]{2,1,0:T(8,128)(2,1)}, u32[]{:S(2)}) %copy-start) | copy-done | bytes 2654232
  124.7 0.0 copy-start.1
  124.7 1.3 copy-done.1
  126.0 0.0 copy-start.2
  126.0 0.9 copy-done.2
  126.9 0.0 copy-start.3
  126.9 0.9 copy-done.3
  127.8 0.0 copy-start.4
  127.8 0.8 copy-done.4
  128.6 0.0 copy-start.5
  128.6 0.7 copy-done.5
  129.4 3.9 %finish.1 = (bf16[1,128,768]{2,1,0:T(8,128)(2,1)}, bf16[1,128,768]{2,1,0:T(8,128)(2,1)}, f32[768]{0:T(1024)}, f32[768]{0:T(1024)}, f32[768]{0:T(1024)}, /*index=...) custom-call(bf16[128,768]{1,0:T(8,128)(2,1)S(1)} %copy-done.2, ...), custom_call_target="tpu_custom_call" | custom-call | tf_op jit(solution)/shard_map/finish/pallas_call | solution.py:1178
Async XLA Ops:
  122.9 1.8 %copy-start = (bf16[2,864,768]{2,1,0:T(8,128)(2,1)S(1)}, bf16[2,864,768]{2,1,0:T(8,128)(2,1)}, u32[]{:S(2)}) copy-start(bf16[2,864,768]{2,1,0:T(8,128)(2,1)} %get-tuple-element.20.fin) | copy-start | bytes 7962628
  124.7 1.3 copy-start.1
  126.0 0.9 copy-start.2
  126.9 0.9 copy-start.3
  127.8 0.8 copy-start.4
  128.6 0.7 copy-start.5

commit v3 on v2

--- a/solution.py
+++ b/solution.py
@@ -357,22 +357,14 @@
     for d in near_planes:
         grad_attn_on(d)
     normed.step(2)
+    for e in mates:
+        arrived(K_POS + e, pos_rx.at[mate(e)])
+    to_scalar = pltpu.make_async_copy(pos_rx, pos_sm, lsem.at[len(loads)])
+    to_scalar.start()
     grad_attn_on(last_plane)
     for k in range(3, Z):
         normed.step(k)
     normed.end()
-    for d in planes:
-        arrived(K_WQ + d, wq.at[pl.ds(at16(plane(d) * rows), rows)])
-
-    @pl.loop(0, ctxs // 2)
-    def _(m):
-        here = pl.ds(at128(m * 2 * block), 2 * block)
-        qkv[pl.ds(2 * m, 2)] = dot(n1[here], wq[...]).reshape(2, block, 384)
-
-    for e in mates:
-        arrived(K_POS + e, pos_rx.at[mate(e)])
-    to_scalar = pltpu.make_async_copy(pos_rx, pos_sm, lsem.at[len(loads)])
-    to_scalar.start()
     to_scalar.wait()
     rank = [lax.div(pos_sm[j, 0, 0], block) for j in range(ctxs)]
     place = []
@@ -381,6 +373,14 @@
         for j in range(1, ctxs):
             found = found + j * (rank[j] == g).astype(jnp.int32)
         place.append(lax.rem(found, ctxs))
+
+    for d in planes:
+        arrived(K_WQ + d, wq.at[pl.ds(at16(plane(d) * rows), rows)])
+
+    @pl.loop(0, ctxs // 2)
+    def _(m):
+        here = pl.ds(at128(m * 2 * block), 2 * block)
+        qkv[pl.ds(2 * m, 2)] = dot(n1[here], wq[...]).reshape(2, block, 384)
 
     lane = lax.broadcasted_iota(jnp.int32, (block, 128), 1)
     leads = lax.rem(lane, HEAD_DIM) < ROTARY // 2
@@ -614,6 +614,14 @@
     go16[pl.ds(2 * HEAD_DIM, HEAD_DIM)] = go[3 * HEAD_DIM :].astype(LOW)
     send(K_GO, go16.at[pl.ds(at16(other * half_rows), half_rows)], go_rx, partner)
 
+    own_gq = gq_tx[my_rows].astype(FULL)
+    for d in planes:
+        arrived(K_GQ + d, gq_rx.at[d])
+        own_gq = own_gq + gq_rx[d].astype(FULL)
+    qkvfin_ref[i] = own_gq.astype(LOW)
+    spread = Relay(lambda j: qkvfin_ref.at[j])
+
+    spread.begin()
     UP = half_width + half_rows
 
     def up_rows(index):
@@ -712,17 +720,10 @@
     for t in reversed(range(1, Z)):
         a1_right(t, low_side)
         a1_left(Z - 1 - t, jnp.logical_not(low_side))
-
-    own_gq = gq_tx[my_rows].astype(FULL)
-    for d in planes:
-        arrived(K_GQ + d, gq_rx.at[d])
-        own_gq = own_gq + gq_rx[d].astype(FULL)
-    qkvfin_ref[i] = own_gq.astype(LOW)
-    spread = Relay(lambda j: qkvfin_ref.at[j])
-
     for t in reversed(range(1, Z)):
         a1_right(t, jnp.logical_not(low_side))
         a1_left(Z - 1 - t, low_side)
+    spread.step(1)
     K_E = channels(ctxs)
     K_EX = channels(shards)
     early_a[3:4] = bias_sum[:, :256]
@@ -731,9 +732,11 @@
         send(K_E + e, early_a, early_rx.at[e], {"ctx": mate(e)})
     early_rx[0] = early_a[...]
 
-    for q in range(4):
+    for q in range(2):
         near_mid(q)
-    spread.begin()
+    spread.step(2)
+    for q in range(2, 4):
+        near_mid(q)
     for d in planes:
         arrived(K_GUX + d, line_own.at[up_rows(plane(d))])
     for q in range(first_up, chunks):
@@ -785,7 +788,6 @@
     for q in range(10, 12):
         near_mid(q)
         far(q - 4)
-    spread.step(1)
     for q in range(12, 15):
         near_mid(q)
         far(q - 4)
@@ -811,7 +813,6 @@
     for d in planes:
         send(K_EX + d, early_b.at[0], early_b.at[d], {"shard": plane(d)})
         send(K_LX + d, late_b.at[0], late_b.at[d], {"shard": plane(d)})
-    spread.step(2)
     for q in range(15, chunks):
         near_mid(q)
         far(q - 4)
@@ -1096,9 +1097,9 @@
 
 
 def finish_body(
-    y_in, dx_in, fin, qkvfin, early, late,
+    y_in, dx_in, fin_in, qkvfin_in, early_in, late_in,
     y_out, dx_out, g1_out, b1_out, g2_out, b2_out, gqkv_out, gqkvb_out, gout_out, gup_out, gupb_out, gdown_out,
-    gqkv, gout, gup, gdown, sem,
+    gqkv, gout, gup, gdown, fin, qkvfin, early, late, y, dx, sem, in_sem,
 ):
     width = y_in.shape[1]
     chips = qkvfin.shape[0] // 2
@@ -1108,23 +1109,46 @@
     shards = width // rows
     slabs = 8 + 4 * chips
     copies = []
+    coming = []
+
+    def bring(src, dst):
+        copy = pltpu.make_async_copy(src, dst, in_sem.at[len(coming)])
+        copy.start()
+        coming.append(copy)
+
+    for h in range(2):
+        bring(fin_in.at[h, pl.ds(0, cut)], fin.at[h, pl.ds(0, cut)])
+    for h in range(2):
+        bring(
+            fin_in.at[h, pl.ds(cut, fin.shape[1] - cut)], fin.at[h, pl.ds(cut, fin.shape[1] - cut)]
+        )
+    bring(qkvfin_in, qkvfin)
+    bring(y_in, y)
+    bring(dx_in, dx)
+    bring(early_in, early)
+    bring(late_in, late)
 
     def out(src, dst):
         copy = pltpu.make_async_copy(src, dst, sem.at[len(copies)])
         copy.start()
         copies.append(copy)
 
-    out(y_in, y_out.at[0])
-    out(dx_in, dx_out.at[0])
     for h in range(2):
+        coming[h].wait()
         gdown[pl.ds(cut * h, cut)] = fin[h, pl.ds(0, cut)].astype(FULL)
         out(gdown.at[pl.ds(cut * h, cut)], gdown_out.at[pl.ds(cut * h, cut)])
     for h in range(2):
+        coming[2 + h].wait()
         mine = pl.ds(half * h, half)
         for n in range(shards):
             here = fin[h, pl.ds(cut + half + half * n, half)]
             gup[mine, width * n : width * (n + 1)] = here.astype(FULL)
         out(gup.at[mine], gup_out.at[mine])
+
+    for copy in coming[4:]:
+        copy.wait()
+    out(y, y_out.at[0])
+    out(dx, dx_out.at[0])
 
     def tiles(piece, wide, put):
         lane = lax.broadcasted_iota(jnp.int32, wide, 1)
@@ -1191,16 +1215,23 @@
             shape((shards * width,), FULL),
             shape((width, width), FULL),
         ),
-        in_specs=[vmem] * 6,
+        in_specs=[hbm] * 6,
         out_specs=(hbm, hbm, vmem, vmem, vmem, vmem, hbm, vmem, hbm, hbm, vmem, hbm),
         scratch_shapes=[
             pltpu.VMEM((rows, 3 * width), FULL),
             pltpu.VMEM((rows, width), FULL),
             pltpu.VMEM((rows, shards * width), FULL),
             pltpu.VMEM((width, width), FULL),
+            pltpu.VMEM(pieces[2].shape, LOW),
+            pltpu.VMEM(pieces[3].shape, LOW),
+            pltpu.VMEM(pieces[4].shape, FULL),
+            pltpu.VMEM(pieces[5].shape, FULL),
+            pltpu.VMEM((block, width), LOW),
+            pltpu.VMEM((block, width), LOW),
             pltpu.SemaphoreType.DMA((8,)),
+            pltpu.SemaphoreType.DMA((16,)),
         ],
-        compiler_params=pltpu.CompilerParams(vmem_limit_bytes=24 * 2**20),
+        compiler_params=pltpu.CompilerParams(vmem_limit_bytes=60 * 1024 * 1024),
         name="finish",
     )(*pieces)
 

time: 134 us -> 124 us (0.925)
  local copies, waits for them, and re-layouts: 6.39 us -> 0 us
  Pallas kernels: 126 us -> 123 us
    unnamed x12 -> x0, local copies, waits for them, and re-layouts: 6.39 us -> none
    pallas_call x1, Pallas kernels: 122 us -> 118 us  [fused_on_device(): pl.pallas_call(functools.partial(fused_body, tuple(scratch)), out_shape=(...]
where the time goes in v3:
time: 124 us
  Pallas kernels  123 us (99%)
    pallas_call x1, Pallas kernels, fused_on_device(): pl.pallas_call(functools.partial(fused_body, tuple(scratch)), out_shape=(...  118 us
    pallas_call x1, Pallas kernels, finish(): pl.pallas_call(finish_body, out_shape=(shape((1, block, width), LOW), sha...  5 us

profile of v3, /device:TPU:0, one launch (start us, length us, event | category | flops | bytes accessed | tf_op | source)
XLA Modules:
  0.0 123.9 jit_solution(11904543684286852451)
XLA Ops:
  0.6 118.1 %layer.1 = (bf16[128,768]{1,0:T(8,128)(2,1)}, bf16[128,768]{1,0:T(8,128)(2,1)}, bf16[2,864,768]{2,1,0:T(8,128)(2,1)}, bf16[8,192,384]{2,1,0:T(8,128)(2,1)}, f32[56,256]{1,0:T(8,128)}, /*index=5*/f32[8,384]{1,0:T(8,128)}) custom-call(bf16[128,768]{1,0:T(8,128)(2,1)} %bitcast.2, s32[1,128]{1,0:T(1,128)} %refs_1_.1, f32[768]{0:T(1024)} %refs_2_.1, ...), custom_call_target="tpu_custom_call" | custom-call | tf_op jit(solution)/shard_map/layer/pallas_call | solution.py:1329
  118.7 5.0 %finish.1 = (bf16[1,128,768]{2,1,0:T(8,128)(2,1)}, bf16[1,128,768]{2,1,0:T(8,128)(2,1)}, f32[768]{0:T(1024)}, f32[768]{0:T(1024)}, f32[768]{0:T(1024)}, /*index=...) custom-call(bf16[128,768]{1,0:T(8,128)(2,1)} %get-tuple-element.18.y, ...), custom_call_target="tpu_custom_call" | custom-call | tf_op jit(solution)/shard_map/finish/pallas_call | solution.py:1202

commit v4 on v3

--- a/solution.py
+++ b/solution.py
@@ -120,8 +120,7 @@
     wq, wraw, wup, wout, wdn, n1, n2, cot, pos_tx, pos_rx, pos_sm, qkv, q_s, k_s, v_s, do_tx, do_mid, do_rx, do_s,
     o_s, dq_s, dk_s, dv_s, gp_s, gp_e, o_tx, o_rx, attn, a1_p, a1_d2d, a1_own, a1_tx_r, a1_tx_l, a1_rx_r, a1_rx_l,
     gq_tx, gq_rx, out_acc, a2_acc, out_tx, out_rx, a2_tx, a2_rx, gd16, gd_rx, gu16, gu_rx, gu_tx,
-    go16, go_rx, line_own, line_rx, line_near, line_far, early_a, early_rx, early_b,
-    late_a, late_rx, late_b, ssem, rsem, lsem,
+    go16, go_rx, line_own, line_rx, line_near, line_far, early_a, early_d2d, early_z, early_x, late_a, late_d2d, late_z, late_x, ssem, rsem, lsem,
 ):
     shards = lax.axis_size("shard")
     ctxs = lax.axis_size("ctx")
@@ -179,6 +178,9 @@
     left = {"ctx": i - 2}
     has_left = z > 0
     has_right = z < Z - 1
+    low_side = z < Z // 2
+    is_end = (z == 0) | (z == Z - 1)
+    is_mid = jnp.logical_not(is_end)
 
     loads = []
 
@@ -210,13 +212,33 @@
                 )
     pl.semaphore_wait(barrier, shards * ctxs - 1)
 
-    K_COT = channels(shards)
+    K_COT = channels(2 * shards)
+    K_N2 = channels(2 * shards)
     K_WQ = channels(shards)
     K_WU = channels(shards)
-    K_WU2 = channels(shards)
-    K_N2 = channels(shards)
     K_POS = channels(ctxs)
-    for d in planes:
+    side, over, across_plane = 1, 2, 3
+    half_block = block // 2
+    part_rows = rows // Z
+    part_cols = width // 2
+
+    def wup_part(owner, j):
+        return wup.at[
+            pl.ds(at16(owner * rows + lax.div(j, 2) * part_rows), part_rows),
+            pl.ds(at128(lax.rem(j, 2) * part_cols), part_cols),
+        ]
+
+    for d in planes:
+        send(
+            K_WU + d,
+            wup_hbm.at[
+                pl.ds(at16(z * part_rows), part_rows),
+                pl.ds(at128(plane(d) * width + c * part_cols), part_cols),
+            ],
+            wup_part(s, i),
+            {"shard": plane(d)},
+        )
+    for d in (side, over):
         send(K_COT + d, cot_hbm, cot.at[pl.ds(block * d, block)], {"shard": plane(d)})
 
     def two_heads(here, there):
@@ -258,8 +280,27 @@
     n1[tokens(i)] = (normal * gain1 + bias1).astype(LOW)
     n2[pl.ds(0, block)] = (normal * gain2 + bias2).astype(LOW)
     pos_rx[i] = pos_tx[...]
+    for d in (side, over):
+        send(K_N2 + d, n2.at[pl.ds(0, block)], n2.at[pl.ds(block * d, block)], {"shard": plane(d)})
     for e in mates:
         send(K_POS + e, pos_tx, pos_rx.at[i], {"ctx": mate(e)})
+
+    def hand_on(k, field):
+        for d, to, half in ((side, over, 0), (over, side, 1)):
+            arrived(k + d, field.at[pl.ds(block * d, block)])
+            send(
+                k + across_plane + half,
+                field.at[pl.ds(block * d + half_block * half, half_block)],
+                field.at[pl.ds(block * across_plane + half_block * half, half_block)],
+                {"shard": plane(to)},
+            )
+
+    def handed_on(k, field):
+        for half in range(2):
+            arrived(
+                k + across_plane + half,
+                field.at[pl.ds(block * across_plane + half_block * half, half_block)],
+            )
 
     class Relay:
         def __init__(self, piece):
@@ -275,31 +316,51 @@
             send(self.to_left, mine, mine, left, self.direct + z, has_left)
             send(self.across, mine, mine, partner, self.across + z)
 
-        def step(self, k):
-            @pl.when(z >= k)
+        def from_left(self, k, here=True):
+            piece = self.piece(i - 2 * k)
+            when = (z >= k) & here
+
+            @pl.when(when)
             def _():
-                arrived(self.direct + z - k, self.piece(i - 2 * k))
-
-            piece = self.piece(i - 2 * k)
+                arrived(self.direct + z - k, piece)
+
             if k < Z - 1:
-                send(self.to_right + k, piece, piece, right, self.direct + z - k, (z >= k) & has_right)
-            send(self.across + 2 * k - 1, piece, piece, partner, self.across + z - k, z >= k)
-
-            @pl.when(z + k < Z)
+                send(self.to_right + k, piece, piece, right, self.direct + z - k, when & has_right)
+            send(self.across + 2 * k - 1, piece, piece, partner, self.across + z - k, when)
+
+        def from_right(self, k, here=True):
+            piece = self.piece(i + 2 * k)
+            when = (z + k < Z) & here
+
+            @pl.when(when)
             def _():
-                arrived(self.direct + z + k, self.piece(i + 2 * k))
-
-            piece = self.piece(i + 2 * k)
+                arrived(self.direct + z + k, piece)
+
             if k < Z - 1:
-                send(self.to_left + k, piece, piece, left, self.direct + z + k, (z + k < Z) & has_left)
-            send(self.across + 2 * k, piece, piece, partner, self.across + z + k, z + k < Z)
+                send(self.to_left + k, piece, piece, left, self.direct + z + k, when & has_left)
+            send(self.across + 2 * k, piece, piece, partner, self.across + z + k, when)
+
+        def step(self, k, here=True):
+            self.from_left(k, here)
+            self.from_right(k, here)
+
+        def step_inner(self, k):
+            self.from_left(k, jnp.logical_not(low_side))
+            self.from_right(k, low_side)
+
+        def step_outer(self, k):
+            self.from_left(k, low_side)
+            self.from_right(k, jnp.logical_not(low_side))
 
         def end(self):
             for to in range(Z):
                 arrived(self.across + to, self.piece(2 * to + other))
 
     normed = Relay(lambda j: n1.at[tokens(j)])
-    normed.begin()
+    ups = [Relay(functools.partial(wup_part, plane(d))) for d in planes]
+    for d in planes:
+        arrived(K_WU + d, wup_part(plane(d), i))
+        ups[d - 1].begin()
     for copy in loads[3:]:
         copy.wait()
 
@@ -308,15 +369,9 @@
     K_DOM = channels(shards)
 
     def grad_attn(d):
-        if d:
-            arrived(K_COT + d, cot.at[pl.ds(block * d, block)])
         field = dot(cot[pl.ds(block * d, block)], wout[...], COLS_CONTRACT)
         for core in range(2):
             do_tx[d, core] = field[:, 128 * core : 128 * (core + 1)].astype(LOW)
-        if d:
-            send(K_DOM + d, do_tx.at[d], do_mid.at[d], {"shard": plane(d)})
-        else:
-            do_mid[0] = do_tx[0]
 
     def grad_attn_on(d):
         if d:
@@ -330,41 +385,170 @@
             def _():
                 do_rx[i] = do_mid[d, core]
 
-    def send_wq(d):
+    grad_attn(0)
+    do_mid[0] = do_tx[0]
+    hand_on(K_COT, cot)
+    grad_attn(side)
+    grad_attn(over)
+    for up in ups:
+        up.step(1)
+    hand_on(K_N2, n2)
+    for up in ups:
+        up.step(2)
+    normed.begin()
+    handed_on(K_COT, cot)
+    grad_attn(across_plane)
+    for d in planes:
+        send(K_DOM + d, do_tx.at[d], do_mid.at[d], {"shard": plane(d)})
+    for d in planes:
         send(K_WQ + d, wq.at[my_rows], wq.at[my_rows], {"shard": plane(d)})
-
-    near_planes, last_plane = planes[:-1], planes[-1]
-    for d in (0, *near_planes):
-        grad_attn(d)
-    for d in near_planes:
-        send_wq(d)
-    normed.step(1)
-    grad_attn_on(0)
-    grad_attn(last_plane)
-    send_wq(last_plane)
-    my_half = pl.ds(at16(s * rows + c * half_rows), half_rows)
-    for d in planes:
-        send(
-            K_WU + d,
-            wup_hbm.at[
-                pl.ds(at16(c * half_rows), half_rows), pl.ds(at128(plane(d) * width), width)
-            ],
-            wup.at[my_half],
-            {"shard": plane(d)},
-        )
-    for d in planes:
-        send(K_N2 + d, n2.at[pl.ds(0, block)], n2.at[pl.ds(block * d, block)], {"shard": plane(d)})
-    for d in near_planes:
-        grad_attn_on(d)
-    normed.step(2)
     for e in mates:
         arrived(K_POS + e, pos_rx.at[mate(e)])
     to_scalar = pltpu.make_async_copy(pos_rx, pos_sm, lsem.at[len(loads)])
     to_scalar.start()
-    grad_attn_on(last_plane)
+    out_acc[...] = jnp.zeros_like(out_acc)
+    a2_acc[...] = jnp.zeros_like(a2_acc)
+    early_a[...] = jnp.zeros_like(early_a)
+    handed_on(K_N2, n2)
+    for up in ups:
+        for k in range(3, Z):
+            up.step(k)
+        up.end()
+    normed.step(1, is_mid)
+
+    @pl.loop(0, width // 256)
+    def _(t):
+        units = pl.ds(at128(t * 256), 256)
+        bias = upb_ref[pl.ds(at128(s * width + t * 256), 256)][None, :]
+        pre = dot(n2[...], wup[:, units]) + bias
+        cdf = 0.5 * (1.0 + lax.erf(pre * INV_ROOT_TWO))
+        hidden = (pre * cdf).astype(LOW)
+        slope = cdf + pre * (jnp.exp(-0.5 * pre * pre) * INV_ROOT_TWO_PI)
+        grad_hidden = dot(cot[...], wdn[units], COLS_CONTRACT)
+        grad_pre = (grad_hidden * slope).astype(LOW)
+        unit_sums = jnp.sum(grad_pre.astype(FULL), axis=0, keepdims=True)
+        early_a[0, pl.ds(t, 1)] = unit_sums[:, :128]
+        early_a[1, pl.ds(t, 1)] = unit_sums[:, 128:]
+        out_acc[...] += dot(hidden, wdn[units])
+        a2_acc[...] += dot(grad_pre, wup[:, units], COLS_CONTRACT)
+        gd16[units] = dot(hidden, cot[...], ROWS_CONTRACT).astype(LOW)
+        gu16[:, units] = dot(n2[...], grad_pre, ROWS_CONTRACT).astype(LOW)
+
+    K_GD = channels(1)
+    K_GU = channels(shards)
+    K_GUX = channels(shards)
+    K_OUT = channels(shards)
+    K_A2 = channels(shards)
+    K_GO = channels(1)
+
+    def rows_of(d, core):
+        return pl.ds(at16(plane(d) * rows + core * half_rows), half_rows)
+
+    send(K_GD, gd16.at[pl.ds(at16(other * half_width), half_width)], gd_rx, partner)
+    for d in (*planes, 0):
+        send(K_GU + d, gu16.at[rows_of(d, other)], gu_rx.at[d], partner)
+    normed.step(1, is_end)
+    grad_attn_on(0)
+    for d in planes:
+        grad_attn_on(d)
+    for d in planes:
+        a2_tx[d] = a2_acc[pl.ds(block * d, block)].astype(LOW)
+
+    is_centre = (z == Z // 2 - 1) | (z == Z // 2)
+    inward = jnp.where(z < Z // 2, 2, -2)
+    inner = {"ctx": i + inward}
+    outer = {"ctx": i - inward}
+    to_inner = jnp.where(is_centre, 1, 0)
+    line_rows = half_width + half_rows + shards * half_rows
+    chunks = line_rows // CHUNK
+    UP = half_width
+    OUT = half_width + shards * half_rows
+    first_up, first_out = UP // CHUNK, OUT // CHUNK
+    K_OUTER = channels(chunks)
+    K_INNER = channels(chunks)
+    K_NEAR = channels(chunks)
+    K_FAR = channels(chunks)
+    K_FIN = channels(chunks)
+
+    def up_rows(index):
+        return pl.ds(at16(UP + index * half_rows), half_rows)
+
+    def span_of(q):
+        return pl.ds(q * CHUNK, CHUNK)
+
+    def near_copy(q, src, k):
+        return copy_of(
+            k + q,
+            K_OUTER + chunks * to_inner + q,
+            src.at[span_of(q)],
+            line_rx.at[to_inner, span_of(q)],
+            inner,
+        )
+
+    def far_copy(q):
+        return copy_of(
+            K_FAR + q, K_INNER + q, line_far.at[span_of(q)], line_rx.at[1, span_of(q)], outer
+        )
+
+    def fin_copy(q):
+        piece = fin_ref.at[c, span_of(q)]
+        return copy_of(K_FIN + q, K_FIN + q, piece, piece, partner)
+
+    def near_end(q):
+        pl.when(is_end)(near_copy(q, line_own, K_NEAR).start)
+
+    def near_mid(q):
+        arrived(K_OUTER + q, line_rx.at[0, span_of(q)])
+        line_near[span_of(q)] = (
+            line_rx[0, span_of(q)].astype(FULL) + line_own[span_of(q)].astype(FULL)
+        ).astype(LOW)
+        near_copy(q, line_near, K_INNER).start()
+
+    def near(q):
+        pl.when(is_mid)(functools.partial(near_mid, q))
+
+    def far(q):
+        arrived(K_INNER + q, line_rx.at[1, span_of(q)])
+        beyond = line_rx[1, span_of(q)].astype(FULL) + line_own[span_of(q)].astype(FULL)
+
+        @pl.when(is_mid)
+        def _():
+            line_far[span_of(q)] = beyond.astype(LOW)
+            far_copy(q).start()
+
+        fin_ref[c, span_of(q)] = (beyond + line_rx[0, span_of(q)].astype(FULL)).astype(LOW)
+        fin_copy(q).start()
+
+    @pl.when(is_end)
+    def _():
+        line_rx[0] = jnp.zeros((line_rows, width), LOW)
+
+    arrived(K_GD, gd_rx)
+    line_own[pl.ds(0, half_width)] = (
+        gd16[pl.ds(at16(c * half_width), half_width)].astype(FULL) + gd_rx[...].astype(FULL)
+    ).astype(LOW)
+    for q in range(first_up):
+        near_end(q)
+    normed.step(2)
+    for d in (*planes, 0):
+        arrived(K_GU + d, gu_rx.at[d])
+        total = (gu16[rows_of(d, c)].astype(FULL) + gu_rx[d].astype(FULL)).astype(LOW)
+        if d:
+            gu_tx[d] = total
+            send(K_GUX + d, gu_tx.at[d], line_own.at[up_rows(s)], {"shard": plane(d)})
+        else:
+            line_own[up_rows(s)] = total
     for k in range(3, Z):
         normed.step(k)
     normed.end()
+    for d in planes:
+        arrived(K_WQ + d, wq.at[pl.ds(at16(plane(d) * rows), rows)])
+
+    @pl.loop(0, ctxs // 2)
+    def _(m):
+        here = pl.ds(at128(m * 2 * block), 2 * block)
+        qkv[pl.ds(2 * m, 2)] = dot(n1[here], wq[...]).reshape(2, block, 384)
+
     to_scalar.wait()
     rank = [lax.div(pos_sm[j, 0, 0], block) for j in range(ctxs)]
     place = []
@@ -373,14 +557,6 @@
         for j in range(1, ctxs):
             found = found + j * (rank[j] == g).astype(jnp.int32)
         place.append(lax.rem(found, ctxs))
-
-    for d in planes:
-        arrived(K_WQ + d, wq.at[pl.ds(at16(plane(d) * rows), rows)])
-
-    @pl.loop(0, ctxs // 2)
-    def _(m):
-        here = pl.ds(at128(m * 2 * block), 2 * block)
-        qkv[pl.ds(2 * m, 2)] = dot(n1[here], wq[...]).reshape(2, block, 384)
 
     lane = lax.broadcasted_iota(jnp.int32, (block, 128), 1)
     leads = lax.rem(lane, HEAD_DIM) < ROTARY // 2
@@ -421,6 +597,8 @@
     dq_s[...] = jnp.zeros_like(dq_s)
     dk_s[...] = jnp.zeros_like(dk_s)
     dv_s[...] = jnp.zeros_like(dv_s)
+
+    slots = {3: 0, 5: 1, 6: 2, 7: 3}
 
     @pl.loop(0, 2)
     def _(h):
@@ -453,6 +631,19 @@
                 dk_s[upto] += dot(grad_score, q_h, ROWS_CONTRACT)
                 dv_s[upto] += dot(prob_low, do_h, ROWS_CONTRACT)
 
+            if g in slots:
+                u = slots[g]
+                pl.when((h == 0) & is_mid)(functools.partial(near_mid, u))
+                pl.when((h == 1) & is_mid)(functools.partial(near_mid, 4 + u))
+                pl.when((h == 1) & is_mid)(functools.partial(far, u))
+
+        @pl.when(h == 0)
+        def _():
+            for d in planes:
+                arrived(K_GUX + d, line_own.at[up_rows(plane(d))])
+            for q in range(first_up, first_out):
+                near_end(q)
+
     K_O = channels(2 * shards)
     K_OS = channels(ctxs)
     for j in range(ctxs):
@@ -476,6 +667,14 @@
         bias_sum = bias_sum + jnp.sum(part.astype(FULL), axis=0, keepdims=True)
     for j in range(ctxs):
         gp_e[pl.ds(block * j, block)] = gp_s[rank[j]]
+    early_a[0, 3:4] = bias_sum[:, 0:128]
+    early_a[1, 3:4] = bias_sum[:, 128:256]
+    early_a[0, 4:5] = bias_sum[:, 256:384]
+    K_ED = channels(1)
+    K_EZ = channels(Z)
+    K_EX = channels(shards)
+    K_EF = channels(1)
+    send(K_ED, early_a.at[other], early_d2d, partner)
 
     @pl.loop(0, ctxs // 2)
     def _(m):
@@ -499,6 +698,8 @@
             K_GQ + d, gq_tx.at[pl.ds(at16(plane(d) * rows), rows)], gq_rx.at[d], {"shard": plane(d)}
         )
 
+    pl.when(is_mid)(functools.partial(far, 4))
+    pl.when(is_mid)(functools.partial(far, 5))
     for t in range(Z):
         arrived(K_A1D + t, a1_d2d.at[t])
         a1_own[t] = (a1_p[2 * t + c].astype(FULL) + a1_d2d[t].astype(FULL)).astype(LOW)
@@ -506,13 +707,11 @@
     K_A1R = channels(Z)
     K_A1L = channels(Z)
 
-    def a1_ends():
-        for t in reversed(range(1, Z)):
-            send(K_A1R + t, a1_own.at[t], a1_rx_r.at[t], right, None, z == 0)
-        for t in range(Z - 1):
-            send(K_A1L + t, a1_own.at[t], a1_rx_l.at[t], left, None, z == Z - 1)
-
-    low_side = z < Z // 2
+    def a1_ends(hops):
+        t = hops
+        send(K_A1R + t, a1_own.at[t], a1_rx_r.at[t], right, None, z == 0)
+        t = Z - 1 - hops
+        send(K_A1L + t, a1_own.at[t], a1_rx_l.at[t], left, None, z == Z - 1)
 
     def a1_right(t, here):
         when = (z > 0) & (z < t) & here
@@ -534,7 +733,8 @@
 
         send(K_A1L + t, a1_tx_l.at[t], a1_rx_l.at[t], left, None, when)
 
-    a1_ends()
+    for hops in reversed(range(1, Z)):
+        a1_ends(hops)
 
     @pl.when(z == 0)
     def _():
@@ -544,50 +744,41 @@
     def _():
         a1_rx_l[Z - 1] = jnp.zeros((block, width), LOW)
 
-    early_a[...] = jnp.zeros_like(early_a)
-    for d in planes:
-        arrived(K_WU + d, wup.at[pl.ds(at16(plane(d) * rows + c * half_rows), half_rows)])
-        part = wup.at[pl.ds(at16(plane(d) * rows + c * half_rows), half_rows)]
-        send(K_WU2 + d, part, part, partner)
-    for d in planes:
-        arrived(K_N2 + d, n2.at[pl.ds(block * d, block)])
-    for d in planes:
-        arrived(K_WU2 + d, wup.at[pl.ds(at16(plane(d) * rows + other * half_rows), half_rows)])
-    out_acc[...] = jnp.zeros_like(out_acc)
-    a2_acc[...] = jnp.zeros_like(a2_acc)
-
-    @pl.loop(0, width // 256)
-    def _(t):
-        units = pl.ds(at128(t * 256), 256)
-        bias = upb_ref[pl.ds(at128(s * width + t * 256), 256)][None, :]
-        pre = dot(n2[...], wup[:, units]) + bias
-        cdf = 0.5 * (1.0 + lax.erf(pre * INV_ROOT_TWO))
-        hidden = (pre * cdf).astype(LOW)
-        slope = cdf + pre * (jnp.exp(-0.5 * pre * pre) * INV_ROOT_TWO_PI)
-        grad_hidden = dot(cot[...], wdn[units], COLS_CONTRACT)
-        grad_pre = (grad_hidden * slope).astype(LOW)
-        early_a[pl.ds(t, 1)] = jnp.sum(grad_pre.astype(FULL), axis=0, keepdims=True)
-        out_acc[...] += dot(hidden, wdn[units])
-        a2_acc[...] += dot(grad_pre, wup[:, units], COLS_CONTRACT)
-        gd16[units] = dot(hidden, cot[...], ROWS_CONTRACT).astype(LOW)
-        gu16[:, units] = dot(n2[...], grad_pre, ROWS_CONTRACT).astype(LOW)
-
-    K_GD = channels(1)
-    K_GU = channels(shards)
-    K_GUX = channels(shards)
-    K_OUT = channels(shards)
-    K_A2 = channels(shards)
-    K_GO = channels(1)
-
-    def rows_of(d, core):
-        return pl.ds(at16(plane(d) * rows + core * half_rows), half_rows)
-
-    for d in range(shards):
-        send(K_GU + d, gu16.at[rows_of(d, other)], gu_rx.at[d], partner)
-    send(K_GD, gd16.at[pl.ds(at16(other * half_width), half_width)], gd_rx, partner)
-    for d in planes:
-        a2_tx[d] = a2_acc[pl.ds(block * d, block)].astype(LOW)
-
+    arrived(K_ED, early_d2d)
+    mine, theirs = early_a[c], early_d2d[...]
+    early_z[0, 0:3] = mine[0:3] + theirs[0:3]
+    even_core = c == 0
+    early_z[0, 3:5] = jnp.where(even_core, mine[3:5], theirs[3:5])
+    early_z[0, 5:7] = jnp.where(even_core, theirs[3:5], mine[3:5])
+    early_z[0, 7:8] = jnp.zeros((1, 128), FULL)
+    for k in range(1, Z):
+        send(K_EZ + k, early_z.at[0], early_z.at[k], {"ctx": mate(2 * k)})
+    near(8)
+    near(9)
+    pl.when(is_mid)(functools.partial(far, 6))
+    pl.when(is_mid)(functools.partial(far, 7))
+    near(10)
+    near(11)
+    pl.when(is_mid)(functools.partial(far, 8))
+    pl.when(is_mid)(functools.partial(far, 9))
+    near(12)
+    near(13)
+    pl.when(is_mid)(functools.partial(far, 10))
+    pl.when(is_mid)(functools.partial(far, 11))
+    near(14)
+    near(15)
+    pl.when(is_mid)(functools.partial(far, 12))
+    pl.when(is_mid)(functools.partial(far, 13))
+    own_gq = gq_tx[my_rows].astype(FULL)
+    for d in planes:
+        arrived(K_GQ + d, gq_rx.at[d])
+        own_gq = own_gq + gq_rx[d].astype(FULL)
+    qkvfin_ref[i] = own_gq.astype(LOW)
+    spread = Relay(lambda j: qkvfin_ref.at[j])
+
+    spread.begin()
+    for d in planes:
+        send(K_A2 + d, a2_tx.at[d], a2_rx.at[d], {"shard": plane(d)})
     for seq in range(shards):
         for core in range(2):
             k = 2 * seq + core
@@ -614,145 +805,33 @@
     go16[pl.ds(2 * HEAD_DIM, HEAD_DIM)] = go[3 * HEAD_DIM :].astype(LOW)
     send(K_GO, go16.at[pl.ds(at16(other * half_rows), half_rows)], go_rx, partner)
 
-    own_gq = gq_tx[my_rows].astype(FULL)
-    for d in planes:
-        arrived(K_GQ + d, gq_rx.at[d])
-        own_gq = own_gq + gq_rx[d].astype(FULL)
-    qkvfin_ref[i] = own_gq.astype(LOW)
-    spread = Relay(lambda j: qkvfin_ref.at[j])
-
-    spread.begin()
-    UP = half_width + half_rows
-
-    def up_rows(index):
-        return pl.ds(at16(UP + index * half_rows), half_rows)
-
-    for d in (*planes, 0):
-        arrived(K_GU + d, gu_rx.at[d])
-        total = (gu16[rows_of(d, c)].astype(FULL) + gu_rx[d].astype(FULL)).astype(LOW)
-        if d:
-            gu_tx[d] = total
-            send(K_GUX + d, gu_tx.at[d], line_own.at[up_rows(s)], {"shard": plane(d)})
-        else:
-            line_own[up_rows(s)] = total
-    for d in planes:
-        send(K_A2 + d, a2_tx.at[d], a2_rx.at[d], {"shard": plane(d)})
     for d in planes:
         send(K_OUT + d, out_tx.at[d], out_rx.at[d], {"shard": plane(d)})
-
-    is_end = (z == 0) | (z == Z - 1)
-    is_mid = jnp.logical_not(is_end)
-    is_centre = (z == Z // 2 - 1) | (z == Z // 2)
-    inward = jnp.where(z < Z // 2, 2, -2)
-    inner = {"ctx": i + inward}
-    outer = {"ctx": i - inward}
-    to_inner = jnp.where(is_centre, 1, 0)
-    line_rows = half_width + half_rows + shards * half_rows
-    chunks = line_rows // CHUNK
-    first_up = UP // CHUNK
-    K_OUTER = channels(chunks)
-    K_INNER = channels(chunks)
-    K_NEAR = channels(chunks)
-    K_FAR = channels(chunks)
-    K_FIN = channels(chunks)
-
-    def span_of(q):
-        return pl.ds(q * CHUNK, CHUNK)
-
-    def near_end(q):
-        send(
-            K_NEAR + q,
-            line_own.at[span_of(q)],
-            line_rx.at[to_inner, span_of(q)],
-            inner,
-            K_OUTER + chunks * to_inner + q,
-            is_end,
-        )
-
-    def near_mid(q):
-        @pl.when(is_mid)
-        def _():
-            arrived(K_OUTER + q, line_rx.at[0, span_of(q)])
-            line_near[span_of(q)] = (
-                line_rx[0, span_of(q)].astype(FULL) + line_own[span_of(q)].astype(FULL)
-            ).astype(LOW)
-
-        send(
-            K_INNER + q,
-            line_near.at[span_of(q)],
-            line_rx.at[to_inner, span_of(q)],
-            inner,
-            K_OUTER + chunks * to_inner + q,
-            is_mid,
-        )
-
-    def far(q):
-        arrived(K_INNER + q, line_rx.at[1, span_of(q)])
-        beyond = line_rx[1, span_of(q)].astype(FULL) + line_own[span_of(q)].astype(FULL)
-
-        @pl.when(is_mid)
-        def _():
-            line_far[span_of(q)] = beyond.astype(LOW)
-
-        send(
-            K_FAR + q, line_far.at[span_of(q)], line_rx.at[1, span_of(q)], outer, K_INNER + q, is_mid
-        )
-        fin_ref[c, span_of(q)] = (beyond + line_rx[0, span_of(q)].astype(FULL)).astype(LOW)
-        send(K_FIN + q, fin_ref.at[c, span_of(q)], fin_ref.at[c, span_of(q)], partner)
-
-    @pl.when(is_end)
-    def _():
-        line_rx[0] = jnp.zeros((line_rows, width), LOW)
-
-    arrived(K_GD, gd_rx)
-    line_own[pl.ds(0, half_width)] = (
-        gd16[pl.ds(at16(c * half_width), half_width)].astype(FULL) + gd_rx[...].astype(FULL)
-    ).astype(LOW)
-    for q in range(half_width // CHUNK):
-        near_end(q)
     arrived(K_GO, go_rx)
-    line_own[pl.ds(half_width, half_rows)] = (
+    line_own[pl.ds(OUT, half_rows)] = (
         go16[pl.ds(at16(c * half_rows), half_rows)].astype(FULL) + go_rx[...].astype(FULL)
     ).astype(LOW)
-    for q in range(half_width // CHUNK, first_up):
+    for q in range(first_out, chunks):
         near_end(q)
-
+    pl.when(is_mid)(functools.partial(far, 14))
+    pl.when(is_mid)(functools.partial(far, 15))
+    spread.step_inner(1)
     for t in reversed(range(1, Z)):
         a1_right(t, low_side)
         a1_left(Z - 1 - t, jnp.logical_not(low_side))
     for t in reversed(range(1, Z)):
         a1_right(t, jnp.logical_not(low_side))
         a1_left(Z - 1 - t, low_side)
-    spread.step(1)
-    K_E = channels(ctxs)
-    K_EX = channels(shards)
-    early_a[3:4] = bias_sum[:, :256]
-    early_a[4:5, 0:128] = bias_sum[:, 256:]
-    for e in mates:
-        send(K_E + e, early_a, early_rx.at[e], {"ctx": mate(e)})
-    early_rx[0] = early_a[...]
-
-    for q in range(2):
-        near_mid(q)
-    spread.step(2)
-    for q in range(2, 4):
-        near_mid(q)
-    for d in planes:
-        arrived(K_GUX + d, line_own.at[up_rows(plane(d))])
-    for q in range(first_up, chunks):
-        near_end(q)
-    near_mid(4)
-    far(0)
-    near_mid(5)
-    far(1)
-    near_mid(6)
-    far(2)
-    near_mid(7)
-    far(3)
-    near_mid(8)
-    far(4)
-    near_mid(9)
-    far(5)
+    for k in range(1, Z):
+        arrived(K_EZ + k, early_z.at[k])
+    early_x[0, 0:8] = sum((early_z[k] for k in range(1, Z)), early_z[0])
+    slabs_end = 8 + 4 * Z
+    for chip in range(Z):
+        early_x[0, 8 + 4 * chip : 12 + 4 * chip] = early_z[flip(z, chip), 3:7]
+    for d in planes:
+        send(K_EX + d, early_x.at[0], early_x.at[d], {"shard": plane(d)})
+    for q in range(first_out):
+        pl.when(is_end)(functools.partial(far, q))
     a1 = a1_own[z].astype(FULL)
 
     @pl.when(has_left)
@@ -771,13 +850,14 @@
     sums = (a1 * normal, a1, a2 * normal, a2)
     for k, field in enumerate(sums):
         total = jnp.sum(field, axis=0, keepdims=True)
-        late_a[2 * k : 2 * k + 1] = total[:, :half_width]
-        late_a[2 * k + 1 : 2 * k + 2] = total[:, half_width:]
-    K_L = channels(ctxs)
+        for n in range(width // 128):
+            at = (k % 2) * (width // 128) + n
+            late_a[k // 2, at : at + 1] = total[:, 128 * n : 128 * (n + 1)]
+    K_LD = channels(1)
+    K_LZ = channels(Z)
     K_LX = channels(shards)
-    for e in mates:
-        send(K_L + e, late_a, late_rx.at[e], {"ctx": mate(e)})
-    late_rx[0] = late_a[...]
+    K_LF = channels(1)
+    send(K_LD, late_a.at[other], late_d2d, partner)
     mixed = a1 * gain1 + a2 * gain2
     back = r * (
         mixed
@@ -785,54 +865,42 @@
         - normal * jnp.mean(mixed * normal, axis=-1, keepdims=True)
     )
     dx_ref[...] = (cot[pl.ds(0, block)].astype(FULL) + back).astype(LOW)
-    for q in range(10, 12):
-        near_mid(q)
-        far(q - 4)
-    for q in range(12, 15):
-        near_mid(q)
-        far(q - 4)
+    spread.step_outer(1)
+    arrived(K_LD, late_d2d)
+    late_z[0] = late_a[c] + late_d2d[...]
+    for k in range(1, Z):
+        send(K_LZ + k, late_z.at[0], late_z.at[k], {"ctx": mate(2 * k)})
+    for q in range(first_out, chunks):
+        near(q)
+    spread.step_inner(2)
+    spread.step_outer(2)
     total = x_ref[...].astype(FULL) + out_acc[pl.ds(0, block)]
     for d in planes:
         arrived(K_OUT + d, out_rx.at[d])
         total = total + out_rx[d].astype(FULL)
     y_ref[...] = total.astype(LOW)
-    for e in mates:
-        arrived(K_E + e, early_rx.at[e])
-    summed = early_rx[0]
-    for e in mates:
-        summed = summed + early_rx[e]
-    early_b[0, 0:8] = summed
-    for j in range(ctxs):
-        early_b[0, 8 + 2 * j : 10 + 2 * j] = early_rx[flip(i, j), 3:5]
-    for e in mates:
-        arrived(K_L + e, late_rx.at[e])
-    summed = late_rx[0]
-    for e in mates:
-        summed = summed + late_rx[e]
-    late_b[0] = summed
-    for d in planes:
-        send(K_EX + d, early_b.at[0], early_b.at[d], {"shard": plane(d)})
-        send(K_LX + d, late_b.at[0], late_b.at[d], {"shard": plane(d)})
-    for q in range(15, chunks):
-        near_mid(q)
-        far(q - 4)
-    for q in range(chunks - 4, chunks):
+    for k in range(1, Z):
+        arrived(K_LZ + k, late_z.at[k])
+    late_x[0] = sum((late_z[k] for k in range(1, Z)), late_z[0])
+    for d in planes:
+        send(K_LX + d, late_x.at[0], late_x.at[d], {"shard": plane(d)})
+    for q in range(first_out, chunks):
         far(q)
-    for d in planes:
-        arrived(K_EX + d, early_b.at[d])
-        arrived(K_LX + d, late_b.at[d])
-    whole = early_b[0]
-    late = late_b[0]
-    for d in planes:
-        whole = whole + early_b[d]
-        late = late + late_b[d]
-    late_ref[...] = late
-    early_ref[0:24] = whole
-    for j in range(shards):
-        early_ref[24 + 8 * j : 32 + 8 * j] = early_b[flip(s, j), 0:8]
     for k in range(3, Z):
         spread.step(k)
+    for d in planes:
+        arrived(K_LX + d, late_x.at[d])
+        arrived(K_EX + d, early_x.at[d])
+    late_ref[c] = sum((late_x[d] for d in planes), late_x[0])
+    early_ref[c, 0:slabs_end] = sum((early_x[d] for d in planes), early_x[0])
+    for j in range(shards):
+        at = slabs_end + 8 * j
+        early_ref[c, at : at + 8] = early_x[flip(s, j), 0:8]
+    send(K_LF, late_ref.at[c], late_ref.at[c], partner)
+    send(K_EF, early_ref.at[c], early_ref.at[c], partner)
     spread.end()
+    arrived(K_LF, late_ref.at[other])
+    arrived(K_EF, early_ref.at[other])
     for q in range(chunks):
         arrived(K_FIN + q, fin_ref.at[other, span_of(q)])
     assert used[0] <= ssem.shape[0]
@@ -841,6 +909,11 @@
             copy.wait_send()
         else:
             pl.when(when)(copy.wait_send)
+    for q in range(chunks):
+        fin_copy(q).wait_send()
+        pl.when(is_end)(near_copy(q, line_own, K_NEAR).wait_send)
+        pl.when(is_mid)(near_copy(q, line_near, K_INNER).wait_send)
+        pl.when(is_mid)(far_copy(q).wait_send)
 
 
 def ring_on_device(
@@ -1141,7 +1214,7 @@
         coming[2 + h].wait()
         mine = pl.ds(half * h, half)
         for n in range(shards):
-            here = fin[h, pl.ds(cut + half + half * n, half)]
+            here = fin[h, pl.ds(cut + half * n, half)]
             gup[mine, width * n : width * (n + 1)] = here.astype(FULL)
         out(gup.at[mine], gup_out.at[mine])
 
@@ -1172,11 +1245,11 @@
     )
     out(gqkv, gqkv_out)
     for h in range(2):
-        gout[pl.ds(half * h, half)] = fin[h, pl.ds(cut, half)].astype(FULL)
+        gout[pl.ds(half * h, half)] = fin[h, pl.ds(cut + half * shards, half)].astype(FULL)
     out(gout, gout_out)
 
     def bias_piece(j, part):
-        row = early[8 + 2 * j + part // 2, 128 * (part % 2) : 128 * (part % 2 + 1)]
+        row = early[part % 2, 8 + 2 * j + part // 2]
         return jnp.broadcast_to(row[None, :], (8, 128))
 
     def put_bias(at, tile):
@@ -1185,10 +1258,11 @@
     tiles(bias_piece, (8, 128), put_bias)
     for n in range(shards):
         for t in range(width // 256):
-            gupb_out[pl.ds(width * n + 256 * t, 256)] = early[slabs + 8 * n + t]
+            for h in range(2):
+                gupb_out[pl.ds(width * n + 256 * t + 128 * h, 128)] = early[h, slabs + 8 * n + t]
     for k, vector in enumerate((g1_out, b1_out, g2_out, b2_out)):
-        vector[pl.ds(0, cut)] = late[2 * k]
-        vector[pl.ds(cut, cut)] = late[2 * k + 1]
+        for n in range(width // 128):
+            vector[pl.ds(128 * n, 128)] = late[k // 2, (k % 2) * (width // 128) + n]
     for copy in copies:
         copy.wait()
 
@@ -1315,17 +1389,19 @@
         line_rx=low(2, line_rows, width),
         line_near=low(line_rows, width),
         line_far=low(line_rows, width),
-        early_a=full(8, 256),
-        early_rx=full(ctxs, 8, 256),
-        early_b=full(shards, 8 + 2 * ctxs, 256),
-        late_a=full(8, width // 2),
-        late_rx=full(ctxs, 8, width // 2),
-        late_b=full(shards, 8, width // 2),
-        ssem=pltpu.SemaphoreType.DMA((320,)),
-        rsem=pltpu.SemaphoreType.DMA((320,)),
+        early_a=full(2, 8, 128),
+        early_d2d=full(8, 128),
+        early_z=full(chips, 8, 128),
+        early_x=full(shards, 8 + 4 * chips, 128),
+        late_a=full(2, width // 64, 128),
+        late_d2d=full(width // 64, 128),
+        late_z=full(chips, width // 64, 128),
+        late_x=full(shards, width // 64, 128),
+        ssem=pltpu.SemaphoreType.DMA((420,)),
+        rsem=pltpu.SemaphoreType.DMA((420,)),
         lsem=pltpu.SemaphoreType.DMA((16,)),
     )
-    slabs = 8 + 2 * ctxs
+    slabs = 8 + 4 * chips
     y, dx, fin, qkvfin, early, late = pl.pallas_call(
         functools.partial(fused_body, tuple(scratch)),
         out_shape=(
@@ -1333,8 +1409,8 @@
             jax.ShapeDtypeStruct((block, width), LOW),
             jax.ShapeDtypeStruct((2, line_rows, width), LOW),
             jax.ShapeDtypeStruct((ctxs, rows, 384), LOW),
-            jax.ShapeDtypeStruct((slabs + 8 * shards, 256), FULL),
-            jax.ShapeDtypeStruct((8, width // 2), FULL),
+            jax.ShapeDtypeStruct((2, slabs + 8 * shards, 128), FULL),
+            jax.ShapeDtypeStruct((2, width // 64, 128), FULL),
         ),
         in_specs=[vmem] * 9 + [hbm] * 5,
         out_specs=(vmem,) * 6,

time: 124 us -> 117 us (0.944)
  Pallas kernels: 123 us -> 116 us
    pallas_call x1, Pallas kernels: 118 us -> 111 us  [fused_on_device(): pl.pallas_call(functools.partial(fused_body, tuple(scratch)), out_shape=(...]
where the time goes in v4:
time: 117 us
  Pallas kernels  116 us (99%)
    pallas_call x1, Pallas kernels, fused_on_device(): pl.pallas_call(functools.partial(fused_body, tuple(scratch)), out_shape=(...  111 us
    pallas_call x1, Pallas kernels, finish(): pl.pallas_call(finish_body, out_shape=(shape((1, block, width), LOW), sha...  5 us

profile of v4, /device:TPU:0, one launch (start us, length us, event | category | flops | bytes accessed | tf_op | source)
XLA Modules:
  0.0 116.5 jit_solution(2101459023316901906)
XLA Ops:
  0.6 110.7 %layer.1 = (bf16[128,768]{1,0:T(8,128)(2,1)}, bf16[128,768]{1,0:T(8,128)(2,1)}, bf16[2,864,768]{2,1,0:T(8,128)(2,1)}, bf16[8,192,384]{2,1,0:T(8,128)(2,1)}, f32[...) custom-call(bf16[128,768]{1,0:T(8,128)(2,1)} %bitcast.2, s32[1,128]{1,0:T(1,128)} %refs_1_.1, f32[768]{0:T(1024)} %refs_2_.1, ...), custom_call_target="tpu_custom_call" | custom-call | tf_op jit(solution)/shard_map/layer/pallas_call | solution.py:1405
  111.4 5.0 %finish.1 = (bf16[1,128,768]{2,1,0:T(8,128)(2,1)}, bf16[1,128,768]{2,1,0:T(8,128)(2,1)}, f32[768]{0:T(1024)}, f32[768]{0:T(1024)}, f32[768]{0:T(1024)}, /*index=...) custom-call(bf16[128,768]{1,0:T(8,128)(2,1)} %get-tuple-element.18.y, ...), custom_call_target="tpu_custom_call" | custom-call | tf_op jit(solution)/shard_map/finish/pallas_call | solution.py:1276
